TPU v7x, 8 devices: a whole 2x2x1 slice. The times are simulated.
8 devices in a mesh: data: 8 (over z, y, x, core).
Axes of the slice: x: 2, y: 2, z: 1, core: 2. Of those that a mesh axis runs over, the one named last changes fastest.
Arguments:
- x_in: bfloat16 [16384, 2048], P('data')
- dy_in: bfloat16 [16384, 2048], P('data')
- weights: bfloat16 [4, 2048, 2048], replicated
- a_old: float32 [8192, 2048], P('data')
- s_old: float32 [8192, 2048], P('data')
- a_inv: float32 [8192, 2048], P('data')
- s_inv: float32 [4, 2048, 2048], replicated
Outputs:
- output 1: float32 [4, 2048, 2048], replicated
- output 2: float32 [8192, 2048], P('data')
- output 3: float32 [8192, 2048], P('data')
All inputs are finite; a program needn't handle non-finite values.
Results may differ from a plain program's by a relative error of at most 0.001.
Values are sent between devices in bfloat16 or wider.
A program may use at most 1 GiB of HBM per device.

v0:
```python
import functools
import jax
import jax.numpy as jnp
from jax import lax
from jax.sharding import PartitionSpec as P

FACTOR_DECAY = 0.75
PRECISE = lax.Precision.HIGHEST


def gelu_grad(pre_act, d_act):
    pullback = jax.vjp(functools.partial(jax.nn.gelu, approximate=True), pre_act.astype(jnp.float32))[1]
    return pullback(d_act.astype(jnp.float32))[0].astype(jnp.bfloat16)


def cross_rows(left_op, right_op):
    return jnp.einsum("bi,bj->ij", left_op, right_op, preferred_element_type=jnp.float32)


def local_pass(x_loc, dy_loc, weights):
    n_layers = weights.shape[0]
    layer_inputs = [x_loc]
    pre_acts = []
    for layer_id in range(n_layers - 1):
        pre_act = jnp.dot(layer_inputs[layer_id], weights[layer_id], preferred_element_type=jnp.float32).astype(jnp.bfloat16)
        pre_acts.append(pre_act)
        layer_inputs.append(jax.nn.gelu(pre_act.astype(jnp.float32), approximate=True).astype(jnp.bfloat16))
    out_grads = [dy_loc] * n_layers
    for layer_id in range(n_layers - 1, 0, -1):
        d_act = jnp.einsum("bj,ij->bi", out_grads[layer_id], weights[layer_id], preferred_element_type=jnp.float32).astype(jnp.bfloat16)
        out_grads[layer_id - 1] = gelu_grad(pre_acts[layer_id - 1], d_act)
    return layer_inputs, out_grads


def solution(mesh):
    n_dev = mesh.shape["data"]

    def device_step(x_loc, dy_loc, weights, a_old_rows, s_old_rows, a_inv_rows, s_inv):
        n_layers = weights.shape[0]
        model_width = weights.shape[1]
        batch_total = x_loc.shape[0] * n_dev
        layer_inputs, out_grads = local_pass(x_loc, dy_loc, weights)
        a_loc = jnp.concatenate([cross_rows(h_in, h_in) for h_in in layer_inputs], axis=0) / batch_total
        s_loc = jnp.concatenate([cross_rows(g_out, g_out) for g_out in out_grads], axis=0) / batch_total
        w_loc = jnp.stack([cross_rows(h_in, g_out) for h_in, g_out in zip(layer_inputs, out_grads)]) / batch_total
        a_sum = lax.psum_scatter(a_loc, "data", scatter_dimension=0, tiled=True)
        s_sum = lax.psum_scatter(s_loc, "data", scatter_dimension=0, tiled=True)
        w_grad = lax.psum(w_loc, "data")
        own_rows = a_old_rows.shape[0]
        layer_id = (lax.axis_index("data") * own_rows) // model_width
        w_grad_own = lax.dynamic_index_in_dim(w_grad, layer_id, axis=0, keepdims=False)
        s_inv_own = lax.dynamic_index_in_dim(s_inv, layer_id, axis=0, keepdims=False)
        left_prod = jnp.dot(a_inv_rows, w_grad_own, precision=PRECISE)
        u_rows = jnp.dot(left_prod, s_inv_own, precision=PRECISE)
        u_full = lax.all_gather(u_rows, "data", axis=0, tiled=True).reshape(n_layers, model_width, model_width)
        a_new = FACTOR_DECAY * a_old_rows + (1.0 - FACTOR_DECAY) * a_sum
        s_new = FACTOR_DECAY * s_old_rows + (1.0 - FACTOR_DECAY) * s_sum
        return u_full, a_new, s_new

    row_spec = P("data", None)
    return jax.shard_map(
        device_step,
        mesh=mesh,
        in_specs=(row_spec, row_spec, P(), row_spec, row_spec, row_spec, P()),
        out_specs=(P(), row_spec, row_spec),
        check_vma=False,
    )
```

profile of v0, /device:TPU:0, one launch (start us, length us, event | category | flops | bytes accessed | tf_op | source)
XLA Modules:
  0.0 2182.0 jit_solution(10884619890052435788)
XLA Ops:
  7.2 0.0 all-reduce.2.cloned.1.call-start
  7.2 22.2 %fusion.55 = bf16[2048,2048]{1,0:T(8,128)(2,1)S(1)} fusion(bf16[2048,2048]{1,0:T(8,128)(2,1)} %param.7, bf16[4,2048,2048]{2,1,0:T(8,128)(2,1)} %param.9), kind=kOutput, calls=%fused_computation.80 | convolution fusion | flops 17184063488 | bytes 25165824 | tf_op jit(solution)/shard_map/dot_general | solution.py:25
  29.4 0.0 copy-start.2
  29.4 3.2 copy-done.2
  32.6 23.7 %fusion.58 = bf16[2048,2048]{1,0:T(8,128)(2,1)S(1)} fusion(bf16[4,2048,2048]{2,1,0:T(8,128)(2,1)} %param.9, bf16[2048,2048]{1,0:T(8,128)(2,1)S(1)} %fusion.55), kind=kOutput, calls=%fused_computation.81 | convolution fusion | flops 17226006528 | bytes 25165824 | tf_op jit(solution)/shard_map/dot_general | solution.py:25
  56.4 0.0 copy-start.4
  56.4 3.2 copy-done.4
  59.6 25.2 %fusion.63 = bf16[2048,2048]{1,0:T(8,128)(2,1)} fusion(bf16[4,2048,2048]{2,1,0:T(8,128)(2,1)} %param.9, bf16[2048,2048]{1,0:T(8,128)(2,1)S(1)} %fusion.58), kind=kOutput, calls=%fused_computation.82 | convolution fusion | flops 17226006528 | bytes 25165824 | tf_op jit(solution)/shard_map/dot_general | solution.py:25
  84.9 0.0 slice-done
  84.9 0.0 slice-done.1
  84.9 31.0 %fusion.5 = bf16[2048,2048]{1,0:T(8,128)(2,1)S(1)} fusion(bf16[2048,2048]{1,0:T(8,128)(2,1)} %fusion.63, bf16[2048,2048]{1,0:T(8,128)(2,1)S(1)} %bitcast.73, bf16[4,2048,2048]{2,1,0:T(8,128)(2,1)} %param.9), kind=kOutput, calls=%fused_computation.26 | convolution fusion | flops 17276338176 | bytes 33554432 | tf_op jit(solution)/shard_map/bj,ij->bi/dot_general | solution.py:30
  115.9 0.0 copy-start
  115.9 0.0 copy-start.3
  115.9 34.4 %fusion.8 = bf16[2048,2048]{1,0:T(8,128)(2,1)S(1)} fusion(bf16[2048,2048]{1,0:T(8,128)(2,1)} %copy-done.4, bf16[2048,2048]{1,0:T(8,128)(2,1)S(1)} %fusion.5, bf16[4,2048,2048]{2,1,0:T(8,128)(2,1)} %param.9), kind=kOutput, calls=%fused_computation.29 | convolution fusion | flops 17276338176 | bytes 33554432 | tf_op jit(solution)/shard_map/bj,ij->bi/dot_general | solution.py:30
  150.3 0.0 copy-done
  150.3 33.9 %fusion.11 = bf16[2048,2048]{1,0:T(8,128)(2,1)} fusion(bf16[2048,2048]{1,0:T(8,128)(2,1)S(1)} %copy-done.3, bf16[2048,2048]{1,0:T(8,128)(2,1)S(1)} %fusion.8, bf16[4,2048,2048]{2,1,0:T(8,128)(2,1)} %param.9), kind=kOutput, calls=%fused_computation.32 | convolution fusion | flops 17276338176 | bytes 33554432 | tf_op jit(solution)/shard_map/bj,ij->bi/dot_general | solution.py:30
  184.2 23.1 %convolution_bitcast_fusion.2 = f32[1,2048,2048]{1,2,0:T(8,128)} fusion(bf16[2048,2048]{1,0:T(8,128)(2,1)S(1)} %fusion.8, bf16[2048,2048]{1,0:T(8,128)(2,1)} %copy-done.2), kind=kOutput, calls=%fused_computation.62 | convolution fusion | flops 17221812224 | bytes 33554432 | tf_op jit(solution)/shard_map/bi,bj->ij/dot_general | solution.py:17
  207.3 25.4 %convolution_bitcast_fusion.1 = f32[1,2048,2048]{1,2,0:T(8,128)} fusion(bf16[2048,2048]{1,0:T(8,128)(2,1)} %copy-done, bf16[2048,2048]{1,0:T(8,128)(2,1)} %copy-done.4), kind=kOutput, calls=%fused_computation.61 | convolution fusion | flops 17221812224 | bytes 33554432 | tf_op jit(solution)/shard_map/bi,bj->ij/dot_general | solution.py:17
  232.7 23.7 %convolution_bitcast_fusion = f32[1,2048,2048]{1,2,0:T(8,128)} fusion(bf16[2048,2048]{1,0:T(8,128)(2,1)S(1)} %bitcast.75, bf16[2048,2048]{1,0:T(8,128)(2,1)} %fusion.63), kind=kOutput, calls=%fused_computation.60 | convolution fusion | flops 17221812224 | bytes 33554432 | tf_op jit(solution)/shard_map/bi,bj->ij/dot_general | solution.py:17
  256.4 24.4 %convolution_bitcast_fusion.3 = f32[1,2048,2048]{1,2,0:T(8,128)} fusion(bf16[2048,2048]{1,0:T(8,128)(2,1)} %fusion.11, bf16[2048,2048]{1,0:T(8,128)(2,1)} %param.7), kind=kOutput, calls=%fused_computation.63 | convolution fusion | flops 17179869184 | bytes 33554432 | tf_op jit(solution)/shard_map/bi,bj->ij/dot_general | solution.py:17
  280.8 44.8 %maximum_multiply_fusion = f32[4,2048,2048]{1,2,0:T(8,128)} fusion(f32[1,2048,2048]{1,2,0:T(8,128)} %convolution_bitcast_fusion, f32[1,2048,2048]{1,2,0:T(8,128)} %convolution_bitcast_fusion.1, f32[1,2048,2048]{1,2,0:T(8,128)} %convolution_bitcast_fusion.2, f32[1,2048,2048]{1,2,0:T(8,128)} %convolution_bitcast_fusion.3), kind=kLoop, calls=%fused_computation | loop fusion | flops 67108864 | bytes 134217728 | tf_op jit(solution)/shard_map/div | solution.py:45
  325.6 0.0 all-reduce.2.cloned.1.call-update
  325.6 0.0 reduce-scatter.5.cloned.1.call-start
  325.6 22.2 %fusion.86 = f32[2048,2048]{1,0:T(8,128)S(1)} fusion(bf16[2048,2048]{1,0:T(8,128)(2,1)} %fusion.11), kind=kOutput, calls=%fused_computation.93 | convolution fusion | flops 17179869184 | bytes 25165824 | tf_op jit(solution)/shard_map/bi,bj->ij/dot_general | solution.py:17
  347.9 0.0 slice-start.4
  347.9 24.5 %fusion.87 = f32[2048,2048]{1,0:T(8,128)} fusion(bf16[2048,2048]{1,0:T(8,128)(2,1)} %copy-done.1), kind=kOutput, calls=%fused_computation.94 | convolution fusion | flops 17179869184 | bytes 25165824 | tf_op jit(solution)/shard_map/bi,bj->ij/dot_general | solution.py:17
  372.4 24.7 %fusion.88 = f32[2048,2048]{1,0:T(8,128)} fusion(bf16[2048,2048]{1,0:T(8,128)(2,1)} %copy-done), kind=kOutput, calls=%fused_computation.95 | convolution fusion | flops 17179869184 | bytes 25165824 | tf_op jit(solution)/shard_map/bi,bj->ij/dot_general | solution.py:17
  397.1 20.5 fusion.89
  417.6 39.9 %maximum_multiply_fusion.2 = f32[8192,2048]{1,0:T(8,128)} fusion(f32[2048,2048]{1,0:T(8,128)} %fusion.89, f32[2048,2048]{1,0:T(8,128)} %fusion.88, f32[2048,2048]{1,0:T(8,128)} %fusion.87, f32[2048,2048]{1,0:T(8,128)S(1)} %fusion.86), kind=kLoop, calls=%fused_computation.2 | loop fusion | flops 67108864 | bytes 134217728 | tf_op jit(solution)/shard_map/div | solution.py:44
  457.5 0.0 reduce-scatter.5.cloned.1.call-update
  457.5 0.0 reduce-scatter.3.cloned.1.call-start
  457.6 24.4 %fusion.85 = f32[2048,2048]{1,0:T(8,128)} fusion(bf16[2048,2048]{1,0:T(8,128)(2,1)} %param.7), kind=kOutput, calls=%fused_computation.92 | convolution fusion | flops 17179869184 | bytes 25165824 | tf_op jit(solution)/shard_map/bi,bj->ij/dot_general | solution.py:17
  482.0 38.6 %fusion.74 = f32[2048,2048]{1,0:T(8,128)} fusion(bf16[2048,2048]{1,0:T(8,128)(2,1)} %fusion.63), kind=kOutput, calls=%fused_computation.89 | convolution fusion | flops 17221812224 | bytes 25165824 | tf_op jit(solution)/shard_map/bi,bj->ij/dot_general | solution.py:17
  520.6 38.7 %fusion.77 = f32[2048,2048]{1,0:T(8,128)} fusion(bf16[2048,2048]{1,0:T(8,128)(2,1)} %copy-done.4), kind=kOutput, calls=%fused_computation.90 | convolution fusion | flops 17221812224 | bytes 25165824 | tf_op jit(solution)/shard_map/bi,bj->ij/dot_general | solution.py:17
  559.4 34.0 %fusion.81 = f32[2048,2048]{1,0:T(8,128)} fusion(bf16[2048,2048]{1,0:T(8,128)(2,1)S(1)} %bitcast.79), kind=kOutput, calls=%fused_computation.91 | convolution fusion | flops 17221812224 | bytes 25165824 | tf_op jit(solution)/shard_map/bi,bj->ij/dot_general | solution.py:17
  593.3 44.9 %maximum_multiply_fusion.1 = f32[8192,2048]{1,0:T(8,128)} fusion(f32[2048,2048]{1,0:T(8,128)} %fusion.74, f32[2048,2048]{1,0:T(8,128)} %fusion.77, f32[2048,2048]{1,0:T(8,128)} %fusion.81, f32[2048,2048]{1,0:T(8,128)} %fusion.85), kind=kLoop, calls=%fused_computation.1 | loop fusion | flops 67108864 | bytes 134217728 | tf_op jit(solution)/shard_map/div | solution.py:43
  638.3 0.0 reduce-scatter.3.cloned.1.call-update
  638.3 0.0 all-gather.2.cloned.1.call-start
  638.3 436.9 %all-reduce.2.cloned.1.call-done = f32[4,2048,2048]{1,2,0:T(8,128)} async-done(((f32[4,2048,2048]{1,2,0:T(8,128)}), f32[4,2048,2048]{1,2,0:T(8,128)}) %all-reduce.2.cloned.1.call-update) | async-done | bytes 67108880 | tf_op jit(solution)/shard_map/psum | solution.py:48
  1075.3 62.8 %fusion.35 = f32[2048,1024]{1,0:T(8,128)S(1)} fusion(f32[1024,2048]{1,0:T(8,128)} %param.12, f32[4,2048,2048]{1,2,0:T(8,128)} %all-reduce.2.cloned.1.call-done, s32[]{:T(128)S(6)} %select_n.11), kind=kOutput, calls=%fused_computation.56 | convolution fusion | flops 51539607552 | bytes 33554436 | tf_op jit(solution)/shard_map/dot_general | solution.py:53
  1138.1 57.3 %fusion.33 = f32[1024,2048]{1,0:T(8,128)} fusion(f32[2048,1024]{1,0:T(8,128)S(1)} %fusion.35, f32[4,2048,2048]{2,1,0:T(8,128)} %param.13, s32[]{:T(128)S(6)} %select_n.11), kind=kOutput, calls=%fused_computation.54 | convolution fusion | flops 51539607552 | bytes 33554436 | tf_op jit(solution)/shard_map/dot_general | solution.py:54
  1195.4 0.0 all-gather.2.cloned.1.call-update
  1195.5 258.0 %reduce-scatter.5.cloned.1.call-done = f32[1024,2048]{1,0:T(8,128)} async-done(((f32[8192,2048]{1,0:T(8,128)}), f32[1024,2048]{1,0:T(8,128)}) %reduce-scatter.5.cloned.1.call-update) | async-done | bytes 8388624 | tf_op jit(solution)/shard_map/reduce_scatter | solution.py:47
  1453.5 12.0 multiply_add_fusion
  1465.5 366.2 %reduce-scatter.3.cloned.1.call-done = f32[1024,2048]{1,0:T(8,128)} async-done(((f32[8192,2048]{1,0:T(8,128)}), f32[1024,2048]{1,0:T(8,128)}) %reduce-scatter.3.cloned.1.call-update) | async-done | bytes 8388624 | tf_op jit(solution)/shard_map/reduce_scatter | solution.py:46
  1831.7 12.0 multiply_add_fusion.1
  1843.8 287.4 %all-gather.2.cloned.1.call-done = f32[8192,2048]{1,0:T(8,128)} async-done(((f32[1024,2048]{1,0:T(8,128)}), f32[8192,2048]{1,0:T(8,128)}) %all-gather.2.cloned.1.call-update) | async-done | bytes 67108880 | tf_op jit(solution)/shard_map/all_gather | solution.py:55
  2131.2 43.8 %copy.18 = f32[4,2048,2048]{2,1,0:T(8,128)} copy(f32[4,2048,2048]{2,1,0:T(8,128)} %bitcast.11) | data formatting | bytes 134217728
  (20 shorter events, 0.0 us)
Async XLA Ops:
  7.2 1068.1 %all-reduce.2.cloned.1.call-start = ((), (), s32[]{:S(2)}) async-start(), calls=%async_computation.2 | async-start | bytes 134217728 | tf_op jit(solution)/shard_map/psum | solution.py:48
  29.4 3.2 copy-start.2
  32.6 52.2 %slice-start = ((s8[8388608]{0:T(1024)(128)(4,1)}), s8[4194304]{0:T(1024)(128)(4,1)S(1)}, s32[]{:S(2)}) async-start(s8[8388608]{0:T(1024)(128)(4,1)} %bitcast.72), calls=%async_computation.6 | async-start | bytes 8388608
  56.4 3.2 copy-start.4
  59.6 25.3 %slice-start.1 = ((s8[8388608]{0:T(1024)(128)(4,1)}), s8[4194304]{0:T(1024)(128)(4,1)S(1)}, s32[]{:S(2)}) async-start(s8[8388608]{0:T(1024)(128)(4,1)} %bitcast.72), calls=%async_computation.7 | async-start | bytes 8388608
  115.9 34.4 %copy-start = (bf16[2048,2048]{1,0:T(8,128)(2,1)}, bf16[2048,2048]{1,0:T(8,128)(2,1)S(1)}, u32[]{:S(2)}) copy-start(bf16[2048,2048]{1,0:T(8,128)(2,1)S(1)} %fusion.5) | copy-start | bytes 25165828
  115.9 34.4 %copy-start.3 = (bf16[2048,2048]{1,0:T(8,128)(2,1)S(1)}, bf16[2048,2048]{1,0:T(8,128)(2,1)}, u32[]{:S(2)}) copy-start(bf16[2048,2048]{1,0:T(8,128)(2,1)} %copy-done.2) | copy-start | bytes 25165828
  150.3 33.9 %copy-start.1 = (bf16[2048,2048]{1,0:T(8,128)(2,1)}, bf16[2048,2048]{1,0:T(8,128)(2,1)S(1)}, u32[]{:S(2)}) copy-start(bf16[2048,2048]{1,0:T(8,128)(2,1)S(1)} %fusion.8) | copy-start | bytes 25165828
  184.2 48.5 %slice-start.2 = ((s8[8388608]{0:T(1024)(128)(4,1)}), s8[4194304]{0:T(1024)(128)(4,1)S(1)}, s32[]{:S(2)}) async-start(s8[8388608]{0:T(1024)(128)(4,1)} %bitcast.74), calls=%async_computation.8 | async-start | bytes 8388608
  207.3 25.4 %slice-start.3 = ((s8[8388608]{0:T(1024)(128)(4,1)}), s8[4194304]{0:T(1024)(128)(4,1)S(1)}, s32[]{:S(2)}) async-start(s8[8388608]{0:T(1024)(128)(4,1)} %bitcast.74), calls=%async_computation.9 | async-start | bytes 8388608
  325.6 1127.9 %reduce-scatter.5.cloned.1.call-start = ((), (), s32[]{:S(2)}) async-start(), calls=%async_computation.5 | async-start | bytes 75497472 | tf_op jit(solution)/shard_map/reduce_scatter | solution.py:47
  347.9 49.2 %slice-start.4 = ((s8[8388608]{0:T(1024)(128)(4,1)}), s8[4194304]{0:T(1024)(128)(4,1)S(1)}, s32[]{:S(2)}) async-start(s8[8388608]{0:T(1024)(128)(4,1)} %bitcast.76), calls=%async_computation.10 | async-start | bytes 8388608
  372.4 24.7 %slice-start.5 = ((s8[8388608]{0:T(1024)(128)(4,1)}), s8[4194304]{0:T(1024)(128)(4,1)S(1)}, s32[]{:S(2)}) async-start(s8[8388608]{0:T(1024)(128)(4,1)} %bitcast.76), calls=%async_computation.11 | async-start | bytes 8388608
  457.5 1374.2 %reduce-scatter.3.cloned.1.call-start = ((), (), s32[]{:S(2)}) async-start(), calls=%async_computation.4 | async-start | bytes 75497472 | tf_op jit(solution)/shard_map/reduce_scatter | solution.py:46
  482.0 77.4 %slice-start.6 = ((s8[8388608]{0:T(1024)(128)(4,1)}), s8[4194304]{0:T(1024)(128)(4,1)S(1)}, s32[]{:S(2)}) async-start(s8[8388608]{0:T(1024)(128)(4,1)} %bitcast.78), calls=%async_computation.12 | async-start | bytes 8388608
  520.6 38.7 %slice-start.7 = ((s8[8388608]{0:T(1024)(128)(4,1)}), s8[4194304]{0:T(1024)(128)(4,1)S(1)}, s32[]{:S(2)}) async-start(s8[8388608]{0:T(1024)(128)(4,1)} %bitcast.78), calls=%async_computation.13 | async-start | bytes 8388608
  638.3 1493.0 %all-gather.2.cloned.1.call-start = ((), (), s32[]{:S(2)}) async-start(), calls=%async_computation.3 | async-start | bytes 75497472 | tf_op jit(solution)/shard_map/all_gather | solution.py:55
Sparse Core Ops, SparseCore 0:
  325.7 749.5 all-reduce.1
  1078.8 374.6 reduce-scatter.4
  1457.0 374.6 reduce-scatter.2
  1834.0 297.2 all-gather.1
where the time goes:
time: 2190 us; the launch traced here: 2180 us
  waiting for transfers between devices  1350 us (62%)
  matrix products  615 us (28%)
  other arithmetic  154 us (7%)
  local copies, waits for them, and re-layouts  50.3 us (2%)
    psum x1, waiting for transfers between devices, device_step(): w_grad = lax.psum(w_loc, 'data')  437 us
    reduce_scatter x1, waiting for transfers between devices, device_step(): a_sum = lax.psum_scatter(a_loc, 'data', scatter_dimension=0, tiled=True)  366 us
    dot_general x12, matrix products, cross_rows(): jnp.einsum('bi,bj->ij', left_op, right_op, preferred_element_type=jnp.flo...  324 us
    all_gather x1, waiting for transfers between devices, device_step(): lax.all_gather(u_rows, 'data', axis=0, tiled=True)  287 us
    reduce_scatter x1, waiting for transfers between devices, device_step(): s_sum = lax.psum_scatter(s_loc, 'data', scatter_dimension=0, tiled=True)  258 us
    dot_general x3, matrix products, local_pass(): jnp.einsum('bj,ij->bi', out_grads[layer_id], weights[layer_id], preferred...  99.3 us
    dot_general x3, matrix products, local_pass(): jnp.dot(layer_inputs[layer_id], weights[layer_id], preferred_element_type...  71.2 us
    dot_general x1, matrix products, device_step(): left_prod = jnp.dot(a_inv_rows, w_grad_own, precision=PRECISE)  62.8 us
  transfers between devices with their start and end apart: 4, of which 4 were waited for; matrix products, arithmetic and copies ran while one was open for 21% of the time, Pallas kernels for 0%

commit v1 on v0

v1 whole, which is shorter than its diff:
```python
import functools
import jax
import jax.numpy as jnp
from jax import lax
from jax.experimental import pallas as pl
from jax.sharding import PartitionSpec as P


FACTOR_DECAY = 0.75
PRECISE = lax.Precision.HIGHEST
HALF_TOP = 32768.0
WIRE = jnp.float16


def gelu_grad(pre_act, d_act):
    pullback = jax.vjp(functools.partial(jax.nn.gelu, approximate=True), pre_act.astype(jnp.float32))[1]
    return pullback(d_act.astype(jnp.float32))[0].astype(jnp.bfloat16)


def cross_rows(left_op, right_op):
    return jnp.einsum("bi,bj->ij", left_op, right_op, preferred_element_type=jnp.float32)


def peak(val):
    return jnp.max(jnp.abs(val)).astype(jnp.float32)


def solution(mesh):
    n_dev = mesh.shape["data"]
    pairs = [[p, p + 1] for p in range(0, n_dev, 2)]

    def hop(val, mask):
        return lax.ppermute(val, "data", [(p, p ^ mask) for p in range(n_dev)])

    def pair_rows(val):
        return lax.all_gather(val, "data", axis_index_groups=pairs, axis=0, tiled=True)

    def device_step(x_loc, dy_loc, weights, a_old_rows, s_old_rows, a_inv_rows, s_inv):
        n_layers, width = weights.shape[0], weights.shape[1]
        batch_total = x_loc.shape[0] * n_dev
        own = a_old_rows.shape[0]
        half = own // 2
        me = lax.axis_index("data")
        chip, core = me // 2, me % 2

        def after(val, *done):
            return lax.optimization_barrier((val,) + done)[0]

        def everywhere(top):
            for mask in (1, 2, 4):
                top = jnp.maximum(top, hop(top, mask))
            return top

        def scale_of(left, right):
            return HALF_TOP / jnp.clip(left * right, 1e-30, 3e38)

        def forward(act, weight):
            pre = jnp.dot(act, weight, preferred_element_type=jnp.float32).astype(jnp.bfloat16)
            act = jax.nn.gelu(pre.astype(jnp.float32), approximate=True).astype(jnp.bfloat16)
            return lax.optimization_barrier((pre, act, peak(act)))

        def backward(grad, weight, pre):
            d_act = jnp.einsum("bj,ij->bi", grad, weight, preferred_element_type=jnp.float32).astype(jnp.bfloat16)
            grad = gelu_grad(pre, d_act)
            return lax.optimization_barrier((grad, peak(grad)))

        def product(left, right, first, rows):
            lhs = lax.dynamic_slice(left, (0, core * own + first), (left.shape[0], rows))
            return cross_rows(lhs, right)

        def chosen(vals, rels):
            def branch(k, vals):
                return tuple(vals[k ^ rel] for rel in rels)

            return lax.switch(chip, [functools.partial(branch, k) for k in range(n_layers)], vals)

        def gathered(vals, rels):
            return {rel: pair_rows(val) for rel, val in zip(rels, lax.optimization_barrier(vals))}

        def partial_sum(operands, scales, rel, first, rows, arrived, done):
            scale = after(scales[chip ^ rel] / batch_total, *done)
            out = product(operands[0][rel], operands[1][rel], first, rows) * scale
            for part in arrived:
                out = out + part.astype(jnp.float32)
            return lax.optimization_barrier(out.astype(WIRE))

        class Routes:
            def __init__(self, operands, scales):
                self.operands, self.scales = operands, scales

            def opposite(self, *done):
                sent_x = partial_sum(self.operands, self.scales, 3, 0, half, (), done)
                sent_y = partial_sum(self.operands, self.scales, 3, half, half, (), (sent_x,))
                self.mid_x, self.mid_y = hop(sent_x, 2), hop(sent_y, 4)
                return sent_y

            def direct(self, *done):
                sent_x = partial_sum(self.operands, self.scales, 1, 0, half, (), done)
                sent_y = partial_sum(self.operands, self.scales, 2, half, half, (), (sent_x,))
                self.near_x, self.near_y = hop(sent_x, 2), hop(sent_y, 4)
                return sent_y

            def joined(self, *done):
                sent_y = partial_sum(self.operands, self.scales, 2, 0, half, (self.mid_x,), done)
                sent_x = partial_sum(self.operands, self.scales, 1, half, half, (self.mid_y,), (sent_y,))
                far_x, far_y = hop(sent_y, 4), hop(sent_x, 2)
                self.parts = ((self.near_x, far_x), (self.near_y, far_y))
                return sent_x

            def whole(self, rel, mask, arrived, *done):
                sent = partial_sum(self.operands, self.scales, rel, 0, own, arrived, done)
                return sent, hop(sent, mask)

            def final(self, old, *done):
                inv = after(1.0 / self.scales[chip], *done)
                wire = [near.astype(jnp.float32) + far.astype(jnp.float32) for near, far in self.parts]
                wire = jnp.concatenate(wire, axis=0) if len(wire) > 1 else wire[0]
                mean = product(self.operands[0][0], self.operands[1][0], 0, own) / batch_total + wire * inv
                if old is not None:
                    mean = FACTOR_DECAY * old + (1.0 - FACTOR_DECAY) * mean
                return lax.optimization_barrier(mean)

        h_peaks = [peak(x_loc)]
        pre_1, act_1, top = forward(x_loc, weights[0])
        h_peaks.append(top)
        pre_2, act_2, top = forward(act_1, weights[1])
        h_peaks.append(top)
        w3_norm = jnp.max(jnp.sum(jnp.abs(weights[2].astype(jnp.float32)), axis=0))
        w2_norm = jnp.max(jnp.sum(jnp.abs(weights[1].astype(jnp.float32)), axis=1))
        h_top = everywhere(jnp.stack(h_peaks))
        h_top = jnp.append(h_top, 1.1 * h_top[2] * w3_norm)
        pre_3, act_3, _ = forward(act_2, weights[2])
        order = (3, 1, 2, 0)
        h_rot = gathered(chosen((x_loc, act_1, act_2, act_3), order), order)
        routes_a = Routes((h_rot, h_rot), scale_of(h_top, h_top))

        g_peaks = [peak(dy_loc)]
        grad_3, top = backward(after(dy_loc, act_3), weights[3], pre_3)
        g_peaks.append(top)
        done, mid = routes_a.whole(3, 2, (), grad_3)
        grad_2, top = backward(after(grad_3, done), weights[2], pre_2)
        g_peaks.append(top)
        g_top = everywhere(jnp.stack(g_peaks[::-1]))
        g_top = jnp.concatenate([(1.25 * g_top[0] * w2_norm)[None], g_top])
        done, near = routes_a.whole(1, 2, (), grad_2)
        grad_1, _ = backward(after(grad_2, done), weights[1], pre_1)
        first_rot = chosen((grad_1, grad_2, grad_3, dy_loc), (3,))
        g_rot = gathered(first_rot, (3,))
        done, far = routes_a.whole(2, 4, (mid,), first_rot[0])
        routes_a.parts = ((near, far),)
        g_rot.update(gathered(chosen(after((grad_1, grad_2, grad_3, dy_loc), done), order[1:]), order[1:]))

        routes_g = Routes((h_rot, g_rot), scale_of(h_top, g_top))
        routes_s = Routes((g_rot, g_rot), scale_of(g_top, g_top))
        done = routes_g.opposite(done)
        done = routes_g.direct(done)
        a_new = routes_a.final(a_old_rows, done)
        done = routes_g.joined(a_new)
        done = routes_s.opposite(done)
        done = routes_s.direct(done)
        g_sum = routes_g.final(None, done)
        s_inv_own = lax.dynamic_index_in_dim(s_inv, chip, axis=0, keepdims=False)
        right = jnp.dot(g_sum, s_inv_own, precision=PRECISE)
        right_other = hop(right, 1)
        done = routes_s.joined(right)

        def encode(val):
            top = jnp.clip(jnp.max(jnp.abs(val)), 1e-30, 3e38)
            power = jnp.clip(jnp.ceil(jnp.log2(top)), -100.0, 128.0)
            code = (val * jnp.exp2(15.0 - power)).astype(WIRE)
            return jnp.concatenate([code, jnp.full((16, width), power, WIRE)], axis=0)

        def blank_kernel(out_ref):
            pass

        u_full = pl.pallas_call(
            blank_kernel,
            out_shape=jax.ShapeDtypeStruct((n_layers, width, width), jnp.float32),
            out_specs=pl.BlockSpec(memory_space=pl.ANY),
        )()

        def place(u_full, part, rel, which, first):
            power = part[half, 0].astype(jnp.float32)
            val = (part[:half].astype(jnp.float32) * jnp.exp2(power - 15.0))[None]
            return lax.dynamic_update_slice(u_full, val, (chip ^ rel, which * own + first, 0))

        coded, prev = [], done
        for first in (0, half):
            inv_own = lax.dynamic_slice(a_inv_rows, (first, core * own), (half, own))
            inv_other = lax.dynamic_slice(a_inv_rows, (first, (1 - core) * own), (half, own))
            u_piece = jnp.dot(inv_own, after(right, prev), precision=PRECISE)
            u_piece = u_piece + jnp.dot(inv_other, after(right_other, u_piece), precision=PRECISE)
            prev = encode(u_piece)
            coded.append(prev)
        from_x = [hop(part, 2) for part in coded]
        from_y = [hop(part, 4) for part in coded]
        diag = [hop(from_x[0], 4), hop(from_y[1], 2)]
        s_new = routes_s.final(s_old_rows, prev)
        for parts, rel in ((coded, 0), (from_x, 1), (from_y, 2), (diag, 3)):
            for part, first in zip(parts, (0, half)):
                u_full = place(u_full, part, rel, core, first)
                u_full = place(u_full, hop(part, 1), rel, 1 - core, first)
        return u_full, a_new, s_new

    row_spec = P("data", None)
    return jax.shard_map(
        device_step,
        mesh=mesh,
        in_specs=(row_spec, row_spec, P(), row_spec, row_spec, row_spec, P()),
        out_specs=(P(), row_spec, row_spec),
        check_vma=False,
    )
```

time: 2190 us -> 1320 us (0.60)
  waiting for transfers between devices: 1350 us -> 400 us
  other arithmetic: 154 us -> 108 us
  starting transfers between devices: 0.16 us -> 42.2 us
  matrix products: 615 us -> 648 us
  local copies, waits for them, and re-layouts: 50.3 us -> 76.4 us
  between operations: 14.4 us -> 40 us
    reduce_scatter x2 -> x0, waiting for transfers between devices: 624 us -> none  [the longest x1 366 us: device_step(): a_sum = lax.psum_scatter(a_loc, 'data', scatter_dimension=0, tiled=True)]
    psum x1 -> x0, waiting for transfers between devices: 437 us -> none  [device_step(): w_grad = lax.psum(w_loc, 'data')]
    ppermute x0 -> x36, waiting for transfers between devices: none -> 398 us  [hop(): return lax.ppermute(val, 'data', [(p, p ^ mask) for p in range(n_dev)])]
    all_gather x1 -> x8, waiting for transfers between devices: 287 us -> 0.09 us  [pair_rows(): lax.all_gather(val, 'data', axis_index_groups=pairs, axis=0, tiled=True)]
    div x3 -> x2, other arithmetic: 130 us -> 0.17 us  [scale_of(): return HALF_TOP / jnp.clip(left * right, 1e-30, 3e+38)]
    cond x0 -> x7, local copies, waits for them, and re-layouts: none -> 58.4 us
    dynamic_update_slice x0 -> x16, other arithmetic: none -> 54.3 us  [place(): lax.dynamic_update_slice(u_full, val, (chip ^ rel, which * own + first, 0))]
    unnamed x27 -> x30, local copies, waits for them, and re-layouts: 50.3 us -> 2.27 us
  transfers between devices with their start and end apart: 4 -> 44, of which waited for: 4 -> 13; matrix products, arithmetic and copies ran while one was open for 21% -> 48% of each run, Pallas kernels for 0% -> 0%
where the time goes in v1:
time: 1320 us; the launch traced here: 1310 us
  matrix products  648 us (49%)
  waiting for transfers between devices  400 us (30%)
  other arithmetic  108 us (8%)
  local copies, waits for them, and re-layouts  76.4 us (6%)
  starting transfers between devices  42.2 us (3%)
  between operations  40 us (3%)
    ppermute x36, waiting for transfers between devices, hop(): return lax.ppermute(val, 'data', [(p, p ^ mask) for p in range(n_dev)])  398 us
    dot_general x18, matrix products, cross_rows(): jnp.einsum('bi,bj->ij', left_op, right_op, preferred_element_type=jnp.flo...  324 us
    dot_general x3, matrix products, backward(): jnp.einsum('bj,ij->bi', grad, weight, preferred_element_type=jnp.float32)  113 us
    dot_general x3, matrix products, forward(): jnp.dot(act, weight, preferred_element_type=jnp.float32)  86.8 us
    cond x7, local copies, waits for them, and re-layouts  58.4 us
    dot_general x1, matrix products, device_step(): right = jnp.dot(g_sum, s_inv_own, precision=PRECISE)  56.5 us
    dynamic_update_slice x16, other arithmetic, place(): lax.dynamic_update_slice(u_full, val, (chip ^ rel, which * own + first, 0))  54.3 us
    ppermute x36, starting transfers between devices, hop(): return lax.ppermute(val, 'data', [(p, p ^ mask) for p in range(n_dev)])  41.5 us
  transfers between devices with their start and end apart: 44, of which 13 were waited for; matrix products, arithmetic and copies ran while one was open for 48% of the time, Pallas kernels for 0%

profile of v1, /device:TPU:0, one launch (start us, length us, event | category | flops | bytes accessed | tf_op | source)
XLA Modules:
  0.0 1314.3 jit_solution(2628667621267339021)
XLA Ops:
  7.2 29.4 %abs_reduce_fusion.7 = (bf16[]{:T(256)}, bf16[2048,2048]{1,0:T(8,128)(2,1)}, bf16[2048,2048]{1,0:T(8,128)(2,1)}) fusion(bf16[2048,2048]{1,0:T(8,128)(2,1)} %param.19, bf16[4,2048,2048]{2,1,0:T(8,128)(2,1)} %param.21), kind=kOutput, calls=%fused_computation.116 | convolution fusion | flops 17234395136 | bytes 33554432 | tf_op jit(solution)/shard_map/dot_general | solution.py:58
  37.2 29.3 %abs_reduce_fusion.6 = (bf16[]{:T(256)}, bf16[2048,2048]{1,0:T(8,128)(2,1)}, bf16[2048,2048]{1,0:T(8,128)(2,1)}) fusion(bf16[2048,2048]{1,0:T(8,128)(2,1)} %get-tuple-element.116, bf16[4,2048,2048]{2,1,0:T(8,128)(2,1)} %param.21), kind=kOutput, calls=%fused_computation.115 | convolution fusion | flops 17234395136 | bytes 33554432 | tf_op jit(solution)/shard_map/dot_general | solution.py:58
  67.1 28.1 %fusion.32 = (bf16[2048,2048]{1,0:T(8,128)(2,1)}, bf16[2048,2048]{1,0:T(8,128)(2,1)}) fusion(bf16[2048,2048]{1,0:T(8,128)(2,1)} %get-tuple-element.117, bf16[4,2048,2048]{2,1,0:T(8,128)(2,1)} %param.21), kind=kOutput, calls=%fused_computation.59 | convolution fusion | flops 17226006528 | bytes 33554432 | tf_op jit(solution)/shard_map/dot_general | solution.py:58
  95.2 33.6 %conditional.3 = (bf16[2048,2048]{1,0:T(8,128)(2,1)}, bf16[2048,2048]{1,0:T(8,128)(2,1)}, bf16[2048,2048]{1,0:T(8,128)(2,1)}, bf16[2048,2048]{1,0:T(8,128)(2,1)}) conditional(s32[]{:T(128)} %clamp.8, (bf16[2048,2048]{1,0:T(8,128)(2,1)}, bf16[2048,2048]{1,0:T(8,128)(2,1)}, bf16[2048,2048]{1,0:T(8,128)(2,1)}, ...), branch_computations={%region_2.3_spmd, %region_3.4_spmd, %region_4.5_spmd, %region_5.6_... | conditional | bytes 67108896 | solution.py:75
  95.2 8.4 copy.10
  103.6 8.4 copy.11
  138.4 38.5 %abs_reduce_fusion.5 = (bf16[]{:T(256)}, bf16[2048,2048]{1,0:T(8,128)(2,1)}) fusion(bf16[2048,2048]{1,0:T(8,128)(2,1)} %get-tuple-element.121, bf16[2048,2048]{1,0:T(8,128)(2,1)} %param.20, bf16[4,2048,2048]{2,1,0:T(8,128)(2,1)} %param.21), kind=kOutput, calls=%fused_computation.113 | convolution fusion | flops 17284726784 | bytes 33554432 | tf_op jit(solution)/shard_map/bj,ij->bi/dot_general | solution.py:63
  177.6 10.4 abs_reduce_fusion
  199.8 26.4 %multiply_convert_fusion.1 = f16[1024,2048]{1,0:T(8,128)(2,1)} fusion(f32[]{:T(128)} %bitcast.9, bf16[4096,2048]{1,0:T(8,128)(2,1)} %all-gather.11.cloned.1.call-done, s32[]{:T(128)S(6)} %select_n.29), kind=kOutput, calls=%fused_computation.109 | convolution fusion | flops 17184063488 | bytes 29360644 | tf_op jit(solution)/shard_map/bi,bj->ij/dot_general | solution.py:21
  226.2 39.2 %abs_reduce_fusion.3 = (bf16[]{:T(256)}, bf16[2048,2048]{1,0:T(8,128)(2,1)}) fusion(bf16[2048,2048]{1,0:T(8,128)(2,1)} %get-tuple-element.128, bf16[2048,2048]{1,0:T(8,128)(2,1)} %get-tuple-element.137, bf16[4,2048,2048]{2,1,0:T(8,128)(2,1)} %param.21), kind=kOutput, calls=%fused_computation.108 | convolution fusion | flops 17284726784 | bytes 33554432 | tf_op jit(solution)/shard_map/bj,ij->bi/dot_general | solution.py:63
  266.1 23.9 %multiply_convert_fusion = f16[1024,2048]{1,0:T(8,128)(2,1)} fusion(f32[]{:T(128)} %bitcast.10, bf16[4096,2048]{1,0:T(8,128)(2,1)} %all-gather.13.cloned.1.call-done, s32[]{:T(128)S(6)} %select_n.29), kind=kOutput, calls=%fused_computation.105 | convolution fusion | flops 17184063488 | bytes 29360644 | tf_op jit(solution)/shard_map/bi,bj->ij/dot_general | solution.py:21
  290.0 35.1 %fusion.11 = bf16[2048,2048]{1,0:T(8,128)(2,1)} fusion(bf16[2048,2048]{1,0:T(8,128)(2,1)} %get-tuple-element.133, bf16[2048,2048]{1,0:T(8,128)(2,1)} %get-tuple-element.136, bf16[4,2048,2048]{2,1,0:T(8,128)(2,1)} %param.21), kind=kOutput, calls=%fused_computation.38 | convolution fusion | flops 17276338176 | bytes 33554432 | tf_op jit(solution)/shard_map/bj,ij->bi/dot_general | solution.py:63
  325.1 8.4 conditional.4
  325.1 8.4 copy.26
  336.3 88.9 %collective-permute-done.3 = f16[1024,2048]{1,0:T(8,128)(2,1)} collective-permute-done((f16[1024,2048]{1,0:T(8,128)(2,1)}, f16[1024,2048]{1,0:T(8,128)(2,1)}, u32[]{:S(2)}, u32[]{:S(2)}) %collective-permute-start.3) | collective-permute-done | bytes 4194336 | tf_op jit(solution)/shard_map/ppermute | solution.py:33
  425.3 24.8 %add_convert_fusion = f16[1024,2048]{1,0:T(8,128)(2,1)} fusion(f16[1024,2048]{1,0:T(8,128)(2,1)} %collective-permute-done.3, f32[]{:T(128)} %bitcast.11, bf16[4096,2048]{1,0:T(8,128)(2,1)} %all-gather.15.cloned.1.call-done, s32[]{:T(128)S(6)} %select_n.29), kind=kOutput, calls=%fused_computation.102 | convolution fusion | flops 17188257792 | bytes 33554948 | tf_op jit(solution)/shard_map/bi,bj->ij/dot_general | solution.py:21
  450.1 16.7 %conditional.5 = (bf16[2048,2048]{1,0:T(8,128)(2,1)}, bf16[2048,2048]{1,0:T(8,128)(2,1)}, bf16[2048,2048]{1,0:T(8,128)(2,1)}) conditional(s32[]{:T(128)} %clamp.8, (bf16[2048,2048]{1,0:T(8,128)(2,1)}, bf16[2048,2048]{1,0:T(8,128)(2,1)}, bf16[2048,2048]{1,0:T(8,128)(2,1)}) %tuple.93, (bf16[2048,2048]{1,0:T(8,128)(2,1)}, ...), branch_computations={%region_15.16_spmd, %region_16.17_spmd, %region_17.18_spmd, %regio... | conditional | bytes 50331672 | solution.py:75
  475.6 10.2 collective-permute-start.8
  485.9 26.6 %fusion.92 = f32[1024,2048]{1,0:T(8,128)} fusion(bf16[4096,2048]{1,0:T(8,128)(2,1)} %all-gather.9.cloned.1.call-done, s32[]{:T(128)S(6)} %select_n.29), kind=kOutput, calls=%fused_computation.121 | convolution fusion | flops 17179869184 | bytes 33554436 | tf_op jit(solution)/shard_map/bi,bj->ij/dot_general | solution.py:21
  512.8 61.7 %collective-permute-done.5 = f32[3]{0:T(128)S(1)} collective-permute-done((f32[3]{0:T(128)S(1)}, f32[3]{0:T(128)S(1)}, u32[]{:S(2)}, u32[]{:S(2)}) %collective-permute-start.5) | collective-permute-done | bytes 44 | tf_op jit(solution)/shard_map/ppermute | solution.py:33
  585.9 16.5 %multiply_convert_fusion.11 = f16[512,2048]{1,0:T(8,128)(2,1)} fusion(bf16[4096,2048]{1,0:T(8,128)(2,1)} %all-gather.21.cloned.1.call-done, bf16[4096,2048]{1,0:T(8,128)(2,1)} %all-gather.11.cloned.1.call-done, s32[]{:T(128)S(6)} %select_n.29, f32[]{:T(128)} %bitcast.18), kind=kOutput, calls=%fused_computation.182 | convolution fusion | flops 8592031744 | bytes 23069188 | tf_op jit(solution)/shard_map/bi,bj->ij/dot_general | solution.py:21
  605.7 11.6 multiply_convert_fusion.10
  617.3 14.8 %multiply_convert_fusion.9 = f16[512,2048]{1,0:T(8,128)(2,1)} fusion(bf16[4096,2048]{1,0:T(8,128)(2,1)} %all-gather.19.cloned.1.call-done, bf16[4096,2048]{1,0:T(8,128)(2,1)} %all-gather.13.cloned.1.call-done, s32[]{:T(128)S(6)} %select_n.29, f32[]{:T(128)} %bitcast.17), kind=kOutput, calls=%fused_computation.180 | convolution fusion | flops 8592031744 | bytes 23069188 | tf_op jit(solution)/shard_map/bi,bj->ij/dot_general | solution.py:21
  632.1 14.7 %multiply_convert_fusion.8 = f16[512,2048]{1,0:T(8,128)(2,1)} fusion(bf16[4096,2048]{1,0:T(8,128)(2,1)} %all-gather.23.cloned.1.call-done, bf16[4096,2048]{1,0:T(8,128)(2,1)} %all-gather.15.cloned.1.call-done, s32[]{:T(128)S(6)} %select_n.34, f32[]{:T(128)} %bitcast.19), kind=kOutput, calls=%fused_computation.175 | convolution fusion | flops 8592031744 | bytes 23069188 | tf_op jit(solution)/shard_map/bi,bj->ij/dot_general | solution.py:21
  650.1 27.8 %collective-permute-done.9 = f16[1024,2048]{1,0:T(8,128)(2,1)} collective-permute-done((f16[1024,2048]{1,0:T(8,128)(2,1)}, f16[1024,2048]{1,0:T(8,128)(2,1)}, u32[]{:S(2)}, u32[]{:S(2)}) %collective-permute-start.9) | collective-permute-done | bytes 4194336 | tf_op jit(solution)/shard_map/ppermute | solution.py:33
  677.9 13.5 %multiply_add_fusion = f32[1024,2048]{1,0:T(8,128)} fusion(f16[1024,2048]{1,0:T(8,128)(2,1)} %collective-permute-done.9, f16[1024,2048]{1,0:T(8,128)(2,1)} %collective-permute-done.8, f32[1024,2048]{1,0:T(8,128)} %fusion.92, f32[1024,2048]{1,0:T(8,128)} %param.22, f32[]{:T(128)} %bitcast.20), kind=kLoop, calls=%fused_computation.100 | loop fusion | flops 18874368 | bytes 33554436 | tf_op jit(solution)/shard_map/add | solution.py:120
  691.4 12.2 add_convert_fusion.4
  705.3 17.6 %collective-permute-done.13 = f16[512,2048]{1,0:T(8,128)(2,1)} collective-permute-done((f16[512,2048]{1,0:T(8,128)(2,1)}, f16[512,2048]{1,0:T(8,128)(2,1)}, u32[]{:S(2)}, u32[]{:S(2)}) %collective-permute-start.13) | collective-permute-done | bytes 2097184 | tf_op jit(solution)/shard_map/ppermute | solution.py:33
  722.9 14.4 %add_convert_fusion.3 = f16[512,2048]{1,0:T(8,128)(2,1)S(1)} fusion(f16[512,2048]{1,0:T(8,128)(2,1)} %collective-permute-done.13, bf16[4096,2048]{1,0:T(8,128)(2,1)} %all-gather.19.cloned.1.call-done, bf16[4096,2048]{1,0:T(8,128)(2,1)} %all-gather.13.cloned.1.call-done, s32[]{:T(128)S(6)} %select_n.34, f32[]{:T(128)} %bitcast.17), kind=kOutput, calls=%fused_computation.170 | convolution fusion | flops 8594128896 | bytes 25166340 | tf_op jit(solution)/shard_map/bi,bj->ij/dot_general | solution.py:21
  739.0 14.6 %multiply_convert_fusion.7 = f16[512,2048]{1,0:T(8,128)(2,1)} fusion(bf16[4096,2048]{1,0:T(8,128)(2,1)} %all-gather.21.cloned.1.call-done, s32[]{:T(128)S(6)} %select_n.29, f32[]{:T(128)} %bitcast.24), kind=kOutput, calls=%fused_computation.160 | convolution fusion | flops 8592031744 | bytes 23069188 | tf_op jit(solution)/shard_map/bi,bj->ij/dot_general | solution.py:21
  753.7 13.6 %multiply_convert_fusion.6 = f16[512,2048]{1,0:T(8,128)(2,1)S(1)} fusion(bf16[4096,2048]{1,0:T(8,128)(2,1)} %all-gather.21.cloned.1.call-done, s32[]{:T(128)S(6)} %select_n.34, f32[]{:T(128)} %bitcast.24), kind=kOutput, calls=%fused_computation.159 | convolution fusion | flops 8592031744 | bytes 23069188 | tf_op jit(solution)/shard_map/bi,bj->ij/dot_general | solution.py:21
  767.3 14.8 %multiply_convert_fusion.5 = f16[512,2048]{1,0:T(8,128)(2,1)} fusion(bf16[4096,2048]{1,0:T(8,128)(2,1)} %all-gather.19.cloned.1.call-done, s32[]{:T(128)S(6)} %select_n.29, f32[]{:T(128)} %bitcast.23), kind=kOutput, calls=%fused_computation.158 | convolution fusion | flops 8592031744 | bytes 23069188 | tf_op jit(solution)/shard_map/bi,bj->ij/dot_general | solution.py:21
  782.1 14.6 %multiply_convert_fusion.4 = f16[512,2048]{1,0:T(8,128)(2,1)} fusion(bf16[4096,2048]{1,0:T(8,128)(2,1)} %all-gather.23.cloned.1.call-done, s32[]{:T(128)S(6)} %select_n.34, f32[]{:T(128)} %bitcast.22), kind=kOutput, calls=%fused_computation.157 | convolution fusion | flops 8592031744 | bytes 23069188 | tf_op jit(solution)/shard_map/bi,bj->ij/dot_general | solution.py:21
  799.6 8.4 collective-permute-done.11
  811.0 23.5 %fusion.51 = f32[1024,2048]{1,0:T(8,128)S(1)} fusion(f32[512,2048]{1,0:T(8,128)} %convert_add_fusion.8, f32[512,2048]{1,0:T(8,128)} %convert_add_fusion.9, f32[]{:T(128)} %bitcast.21, bf16[4096,2048]{1,0:T(8,128)(2,1)} %all-gather.17.cloned.1.call-done, bf16[4096,2048]{1,0:T(8,128)(2,1)} %all-gather.9.cloned.1.call-done, s32[]{:T(128)S(6)} %select_n.29), kind=kOutput, calls=%fused_computation.81 | convolution fusion | flops 17188257792 | bytes 41943556 | tf_op jit(solution)/shard_map/bi,bj->ij/dot_general | solution.py:21
  834.5 56.5 %fusion.48 = f32[1024,2048]{1,0:T(8,128)} fusion(f32[1024,2048]{1,0:T(8,128)S(1)} %fusion.51, f32[4,2048,2048]{2,1,0:T(8,128)} %param.25, s32[]{:T(128)S(6)} %select_n.36), kind=kOutput, calls=%fused_computation.75 | convolution fusion | flops 51539607552 | bytes 33554436 | tf_op jit(solution)/shard_map/dot_general | solution.py:163
  895.0 44.8 %collective-permute-done.15 = f16[512,2048]{1,0:T(8,128)(2,1)} collective-permute-done((f16[512,2048]{1,0:T(8,128)(2,1)}, f16[512,2048]{1,0:T(8,128)(2,1)}, u32[]{:S(2)}, u32[]{:S(2)}) %collective-permute-start.15) | collective-permute-done | bytes 2097184 | tf_op jit(solution)/shard_map/ppermute | solution.py:33
  939.8 15.6 %add_convert_fusion.2 = f16[512,2048]{1,0:T(8,128)(2,1)} fusion(f16[512,2048]{1,0:T(8,128)(2,1)} %collective-permute-done.15, bf16[4096,2048]{1,0:T(8,128)(2,1)} %all-gather.23.cloned.1.call-done, s32[]{:T(128)S(6)} %select_n.29, f32[]{:T(128)} %bitcast.22), kind=kOutput, calls=%fused_computation.152 | convolution fusion | flops 8594128896 | bytes 25166340 | tf_op jit(solution)/shard_map/bi,bj->ij/dot_general | solution.py:21
  955.4 15.1 %add_convert_fusion.1 = f16[512,2048]{1,0:T(8,128)(2,1)} fusion(f16[512,2048]{1,0:T(8,128)(2,1)} %collective-permute-done.16, bf16[4096,2048]{1,0:T(8,128)(2,1)} %all-gather.19.cloned.1.call-done, s32[]{:T(128)S(6)} %select_n.34, f32[]{:T(128)} %bitcast.23), kind=kOutput, calls=%fused_computation.151 | convolution fusion | flops 8594128896 | bytes 25166340 | tf_op jit(solution)/shard_map/bi,bj->ij/dot_general | solution.py:21
  973.3 16.2 %fusion.162 = f32[512,2048]{1,0:T(8,128)S(1)} fusion(f32[1024,2048]{1,0:T(8,128)} %fusion.48, f32[1024,2048]{1,0:T(8,128)S(1)} %bitcast.147, s32[]{:T(128)S(6)} %select_n.29), kind=kOutput, calls=%fused_computation.195 | convolution fusion | flops 12884901888 | bytes 14680068 | tf_op jit(solution)/shard_map/dot_general | solution.py:191
  989.6 17.7 %abs_reduce_fusion.9 = (f32[]{:T(128)}, f32[512,2048]{1,0:T(8,128)}) fusion(f32[512,2048]{1,0:T(8,128)S(1)} %fusion.162, f32[1024,2048]{1,0:T(8,128)} %collective-permute-done.17, f32[1024,2048]{1,0:T(8,128)S(1)} %bitcast.147, s32[]{:T(128)S(6)} %select_n.37), kind=kOutput, calls=%fused_computation.150 | convolution fusion | flops 12888047616 | bytes 18874376 | tf_op jit(solution)/shard_map/dot_general | solution.py:192
  1015.2 13.9 %collective-permute-done.35 = f16[512,2048]{1,0:T(8,128)(2,1)} collective-permute-done((f16[512,2048]{1,0:T(8,128)(2,1)}, f16[512,2048]{1,0:T(8,128)(2,1)}, u32[]{:S(2)}, u32[]{:S(2)}) %collective-permute-start.35) | collective-permute-done | bytes 2097184 | tf_op jit(solution)/shard_map/ppermute | solution.py:33
  1041.2 35.3 %collective-permute-done.24 = f16[528,2048]{1,0:T(8,128)(2,1)} collective-permute-done((f16[528,2048]{1,0:T(8,128)(2,1)S(1)}, f16[528,2048]{1,0:T(8,128)(2,1)}, u32[]{:S(2)}, u32[]{:S(2)}) %collective-permute-start.24) | collective-permute-done | bytes 2162720 | tf_op jit(solution)/shard_map/ppermute | solution.py:33
  1076.5 16.1 %fusion.159 = f32[512,2048]{1,0:T(8,128)S(1)} fusion(f32[1024,2048]{1,0:T(8,128)} %fusion.48, f32[1024,2048]{1,0:T(8,128)S(1)} %bitcast.149, s32[]{:T(128)S(6)} %select_n.29), kind=kOutput, calls=%fused_computation.192 | convolution fusion | flops 12884901888 | bytes 14680068 | tf_op jit(solution)/shard_map/dot_general | solution.py:191
  1092.6 17.7 %abs_reduce_fusion.8 = (f32[]{:T(128)}, f32[512,2048]{1,0:T(8,128)}) fusion(f32[512,2048]{1,0:T(8,128)S(1)} %fusion.159, f32[1024,2048]{1,0:T(8,128)} %collective-permute-done.17, f32[1024,2048]{1,0:T(8,128)S(1)} %bitcast.149, s32[]{:T(128)S(6)} %select_n.37), kind=kOutput, calls=%fused_computation.148 | convolution fusion | flops 12888047616 | bytes 18874376 | tf_op jit(solution)/shard_map/dot_general | solution.py:192
  1127.4 25.9 %fusion.54 = f32[1024,2048]{1,0:T(8,128)} fusion(f32[512,2048]{1,0:T(8,128)S(1)} %copy-done.1, f32[512,2048]{1,0:T(8,128)S(1)} %copy-done.2, f32[1024,2048]{1,0:T(8,128)} %param.23, f32[]{:T(128)} %bitcast.56, bf16[4096,2048]{1,0:T(8,128)(2,1)} %all-gather.17.cloned.1.call-done, s32[]{:T(128)S(6)} %select_n.29), kind=kOutput, calls=%fused_computation.85 | convolution fusion | flops 17194549248 | bytes 50332164 | tf_op jit(solution)/shard_map/bi,bj->ij/dot_general | solution.py:21
  1155.2 61.4 %collective-permute-done.28 = f16[528,2048]{1,0:T(8,128)(2,1)S(1)} collective-permute-done((f16[528,2048]{1,0:T(8,128)(2,1)}, f16[528,2048]{1,0:T(8,128)(2,1)S(1)}, u32[]{:S(2)}, u32[]{:S(2)}) %collective-permute-start.28) | collective-permute-done | bytes 2162720 | tf_op jit(solution)/shard_map/ppermute | solution.py:33
  1242.0 32.5 %collective-permute-done.30 = f16[528,2048]{1,0:T(8,128)(2,1)S(1)} collective-permute-done((f16[528,2048]{1,0:T(8,128)(2,1)}, f16[528,2048]{1,0:T(8,128)(2,1)S(1)}, u32[]{:S(2)}, u32[]{:S(2)}) %collective-permute-start.30) | collective-permute-done | bytes 2162720 | tf_op jit(solution)/shard_map/ppermute | solution.py:33
  (176 shorter events, 174.8 us)
Async XLA Ops:
  7.2 192.6 %all-gather.11.cloned.1.call-start = ((), (), s32[]{:S(2)}) async-start(), calls=%async_computation.1 | async-start | bytes 25165824 | tf_op jit(solution)/shard_map/all_gather | solution.py:36
  128.8 137.3 %all-gather.13.cloned.1.call-start = ((), (), s32[]{:S(2)}) async-start(), calls=%async_computation.2 | async-start | bytes 25165824 | tf_op jit(solution)/shard_map/all_gather | solution.py:36
  129.6 206.7 %all-gather.15.cloned.1.call-start = ((), (), s32[]{:S(2)}) async-start(), calls=%async_computation.3 | async-start | bytes 25165824 | tf_op jit(solution)/shard_map/all_gather | solution.py:36
  130.3 355.6 %all-gather.9.cloned.1.call-start = ((), (), s32[]{:S(2)}) async-start(), calls=%async_computation | async-start | bytes 25165824 | tf_op jit(solution)/shard_map/all_gather | solution.py:36
  137.0 51.5 %collective-permute-start = (f32[3]{0:T(128)S(1)}, f32[3]{0:T(128)S(1)}, u32[]{:S(2)}, u32[]{:S(2)}) collective-permute-start(f32[3]{0:T(128)S(1)} %pad_maximum_fusion), channel_id=1, source_target_pairs={{0,1},{1,0},{2,3},{3,2},{4,5},{5,4},{6,7},{7,6}} | collective-permute-start | bytes 44 | tf_op jit(solution)/shard_map/ppermute | solution.py:33
  137.9 448.0 %all-gather.21.cloned.1.call-start = ((), (), s32[]{:S(2)}) async-start(), calls=%async_computation.6 | async-start | bytes 25165824 | tf_op jit(solution)/shard_map/all_gather | solution.py:36
  188.6 3.6 collective-permute-start.1
  192.3 3.6 collective-permute-start.2
  333.6 283.7 %all-gather.19.cloned.1.call-start = ((), (), s32[]{:S(2)}) async-start(), calls=%async_computation.5 | async-start | bytes 25165824 | tf_op jit(solution)/shard_map/all_gather | solution.py:36
  333.6 91.6 %collective-permute-start.3 = (f16[1024,2048]{1,0:T(8,128)(2,1)}, f16[1024,2048]{1,0:T(8,128)(2,1)}, u32[]{:S(2)}, u32[]{:S(2)}) collective-permute-start(f16[1024,2048]{1,0:T(8,128)(2,1)} %multiply_convert_fusion.1), channel_id=1, source_target_pairs={{0,2},{1,3},{2,0},{3,1},{4,6},{5,7},{6,4},{7,5}} | collective-permute-start | bytes 12582920 | tf_op jit(solution)/shard_map/ppermute | solution.py:33
  466.9 165.2 %all-gather.23.cloned.1.call-start = ((), (), s32[]{:S(2)}) async-start(), calls=%async_computation.7 | async-start | bytes 25165824 | tf_op jit(solution)/shard_map/all_gather | solution.py:36
  467.6 343.3 %all-gather.17.cloned.1.call-start = ((), (), s32[]{:S(2)}) async-start(), calls=%async_computation.4 | async-start | bytes 25165824 | tf_op jit(solution)/shard_map/all_gather | solution.py:36
  475.6 173.1 %collective-permute-start.8 = (f16[1024,2048]{1,0:T(8,128)(2,1)}, f16[1024,2048]{1,0:T(8,128)(2,1)}, u32[]{:S(2)}, u32[]{:S(2)}) collective-permute-start(f16[1024,2048]{1,0:T(8,128)(2,1)} %multiply_convert_fusion), channel_id=1, source_target_pairs={{0,2},{1,3},{2,0},{3,1},{4,6},{5,7},{6,4},{7,5}} | collective-permute-start | bytes 12582920 | tf_op jit(solution)/shard_map/ppermute | solution.py:33
  485.9 93.0 %copy-start.5 = (f32[3]{0:T(128)S(1)}, f32[3]{0:T(128)}, u32[]{:S(2)}) copy-start(f32[3]{0:T(128)} %copy-done.4) | copy-start | bytes 40
  485.9 26.6 %collective-permute-start.4 = (f32[3]{0:T(128)S(1)}, f32[3]{0:T(128)S(1)}, u32[]{:S(2)}, u32[]{:S(2)}) collective-permute-start(f32[3]{0:T(128)S(1)} %pad_maximum_fusion.2), channel_id=1, source_target_pairs={{0,1},{1,0},{2,3},{3,2},{4,5},{5,4},{6,7},{7,6}} | collective-permute-start | bytes 44 | tf_op jit(solution)/shard_map/ppermute | solution.py:33
  512.6 62.0 %collective-permute-start.5 = (f32[3]{0:T(128)S(1)}, f32[3]{0:T(128)S(1)}, u32[]{:S(2)}, u32[]{:S(2)}) collective-permute-start(f32[3]{0:T(128)S(1)} %fusion.221), channel_id=1, source_target_pairs={{0,2},{1,3},{2,0},{3,1},{4,6},{5,7},{6,4},{7,5}} | collective-permute-start | bytes 44 | tf_op jit(solution)/shard_map/ppermute | solution.py:33
  574.6 3.6 collective-permute-start.6
  584.1 93.8 %collective-permute-start.9 = (f16[1024,2048]{1,0:T(8,128)(2,1)}, f16[1024,2048]{1,0:T(8,128)(2,1)}, u32[]{:S(2)}, u32[]{:S(2)}) collective-permute-start(f16[1024,2048]{1,0:T(8,128)(2,1)} %add_convert_fusion), channel_id=1, source_target_pairs={{0,4},{1,5},{2,6},{3,7},{4,0},{5,1},{6,2},{7,3}} | collective-permute-start | bytes 12582920 | tf_op jit(solution)/shard_map/ppermute | solution.py:33
  602.4 88.9 %collective-permute-start.10 = (f16[512,2048]{1,0:T(8,128)(2,1)}, f16[512,2048]{1,0:T(8,128)(2,1)}, u32[]{:S(2)}, u32[]{:S(2)}) collective-permute-start(f16[512,2048]{1,0:T(8,128)(2,1)} %multiply_convert_fusion.11), channel_id=1, source_target_pairs={{0,2},{1,3},{2,0},{3,1},{4,6},{5,7},{6,4},{7,5}} | collective-permute-start | bytes 6291464 | tf_op jit(solution)/shard_map/ppermute | solution.py:33
  617.3 105.6 %collective-permute-start.13 = (f16[512,2048]{1,0:T(8,128)(2,1)}, f16[512,2048]{1,0:T(8,128)(2,1)}, u32[]{:S(2)}, u32[]{:S(2)}) collective-permute-start(f16[512,2048]{1,0:T(8,128)(2,1)} %multiply_convert_fusion.10), channel_id=1, source_target_pairs={{0,4},{1,5},{2,6},{3,7},{4,0},{5,1},{6,2},{7,3}} | collective-permute-start | bytes 6291464 | tf_op jit(solution)/shard_map/ppermute | solution.py:33
  646.8 150.0 %collective-permute-start.12 = (f16[512,2048]{1,0:T(8,128)(2,1)}, f16[512,2048]{1,0:T(8,128)(2,1)S(1)}, u32[]{:S(2)}, u32[]{:S(2)}) collective-permute-start(f16[512,2048]{1,0:T(8,128)(2,1)} %multiply_convert_fusion.8), channel_id=1, source_target_pairs={{0,4},{1,5},{2,6},{3,7},{4,0},{5,1},{6,2},{7,3}} | collective-permute-start | bytes 6291464 | tf_op jit(solution)/shard_map/ppermute | solution.py:33
  648.8 42.6 %slice-start.6 = ((s8[16777216]{0:T(1024)(128)(4,1)}), s8[4194304]{0:T(1024)(128)(4,1)S(1)}, s32[]{:S(2)}) async-start(s8[16777216]{0:T(1024)(128)(4,1)} %bitcast.151), calls=%async_computation.14 | async-start | bytes 8388608
  648.8 42.6 %slice-start.7 = ((s8[16777216]{0:T(1024)(128)(4,1)}), s8[4194304]{0:T(1024)(128)(4,1)S(1)}, s32[]{:S(2)}) async-start(s8[16777216]{0:T(1024)(128)(4,1)} %bitcast.151), calls=%async_computation.15 | async-start | bytes 8388608
  648.8 150.8 %collective-permute-start.7 = (f16[512,2048]{1,0:T(8,128)(2,1)}, f16[512,2048]{1,0:T(8,128)(2,1)S(1)}, u32[]{:S(2)}, u32[]{:S(2)}) collective-permute-start(f16[512,2048]{1,0:T(8,128)(2,1)} %multiply_convert_fusion.9), channel_id=1, source_target_pairs={{0,2},{1,3},{2,0},{3,1},{4,6},{5,7},{6,4},{7,5}} | collective-permute-start | bytes 6291464 | tf_op jit(solution)/shard_map/ppermute | solution.py:33
  703.6 104.5 %collective-permute-start.11 = (f16[512,2048]{1,0:T(8,128)(2,1)}, f16[512,2048]{1,0:T(8,128)(2,1)S(1)}, u32[]{:S(2)}, u32[]{:S(2)}) collective-permute-start(f16[512,2048]{1,0:T(8,128)(2,1)} %add_convert_fusion.4), channel_id=1, source_target_pairs={{0,4},{1,5},{2,6},{3,7},{4,0},{5,1},{6,2},{7,3}} | collective-permute-start | bytes 6291464 | tf_op jit(solution)/shard_map/ppermute | solution.py:33
  737.3 59.5 %collective-permute-start.14 = (f16[512,2048]{1,0:T(8,128)(2,1)S(1)}, f16[512,2048]{1,0:T(8,128)(2,1)S(1)}, u32[]{:S(2)}, u32[]{:S(2)}) collective-permute-start(f16[512,2048]{1,0:T(8,128)(2,1)S(1)} %add_convert_fusion.3), channel_id=1, source_target_pairs={{0,2},{1,3},{2,0},{3,1},{4,6},{5,7},{6,4},{7,5}} | collective-permute-start | bytes 6291464 | tf_op jit(solution)/shard_map/ppermute | solution.py:33
  891.0 98.6 %collective-permute-start.17 = (f32[1024,2048]{1,0:T(8,128)}, f32[1024,2048]{1,0:T(8,128)}, u32[]{:S(2)}, u32[]{:S(2)}) collective-permute-start(f32[1024,2048]{1,0:T(8,128)} %fusion.48), channel_id=1, source_target_pairs={{0,1},{1,0},{2,3},{3,2},{4,5},{5,4},{6,7},{7,6}} | collective-permute-start | bytes 25165832 | tf_op jit(solution)/shard_map/ppermute | solution.py:33
  891.0 48.8 %collective-permute-start.15 = (f16[512,2048]{1,0:T(8,128)(2,1)}, f16[512,2048]{1,0:T(8,128)(2,1)}, u32[]{:S(2)}, u32[]{:S(2)}) collective-permute-start(f16[512,2048]{1,0:T(8,128)(2,1)} %multiply_convert_fusion.7), channel_id=1, source_target_pairs={{0,2},{1,3},{2,0},{3,1},{4,6},{5,7},{6,4},{7,5}} | collective-permute-start | bytes 6291464 | tf_op jit(solution)/shard_map/ppermute | solution.py:33
  892.4 63.0 %collective-permute-start.16 = (f16[512,2048]{1,0:T(8,128)(2,1)S(1)}, f16[512,2048]{1,0:T(8,128)(2,1)}, u32[]{:S(2)}, u32[]{:S(2)}) collective-permute-start(f16[512,2048]{1,0:T(8,128)(2,1)S(1)} %multiply_convert_fusion.6), channel_id=1, source_target_pairs={{0,4},{1,5},{2,6},{3,7},{4,0},{5,1},{6,2},{7,3}} | collective-permute-start | bytes 6291464 | tf_op jit(solution)/shard_map/ppermute | solution.py:33
  893.7 121.5 %collective-permute-start.34 = (f16[512,2048]{1,0:T(8,128)(2,1)}, f16[512,2048]{1,0:T(8,128)(2,1)}, u32[]{:S(2)}, u32[]{:S(2)}) collective-permute-start(f16[512,2048]{1,0:T(8,128)(2,1)} %multiply_convert_fusion.4), channel_id=1, source_target_pairs={{0,4},{1,5},{2,6},{3,7},{4,0},{5,1},{6,2},{7,3}} | collective-permute-start | bytes 6291464 | tf_op jit(solution)/shard_map/ppermute | solution.py:33
  894.4 140.0 %collective-permute-start.32 = (f16[512,2048]{1,0:T(8,128)(2,1)}, f16[512,2048]{1,0:T(8,128)(2,1)}, u32[]{:S(2)}, u32[]{:S(2)}) collective-permute-start(f16[512,2048]{1,0:T(8,128)(2,1)} %multiply_convert_fusion.5), channel_id=1, source_target_pairs={{0,2},{1,3},{2,0},{3,1},{4,6},{5,7},{6,4},{7,5}} | collective-permute-start | bytes 6291464 | tf_op jit(solution)/shard_map/ppermute | solution.py:33
  970.5 58.6 %collective-permute-start.35 = (f16[512,2048]{1,0:T(8,128)(2,1)}, f16[512,2048]{1,0:T(8,128)(2,1)}, u32[]{:S(2)}, u32[]{:S(2)}) collective-permute-start(f16[512,2048]{1,0:T(8,128)(2,1)} %add_convert_fusion.1), channel_id=1, source_target_pairs={{0,2},{1,3},{2,0},{3,1},{4,6},{5,7},{6,4},{7,5}} | collective-permute-start | bytes 6291464 | tf_op jit(solution)/shard_map/ppermute | solution.py:33
  972.0 62.5 %collective-permute-start.33 = (f16[512,2048]{1,0:T(8,128)(2,1)}, f16[512,2048]{1,0:T(8,128)(2,1)}, u32[]{:S(2)}, u32[]{:S(2)}) collective-permute-start(f16[512,2048]{1,0:T(8,128)(2,1)} %add_convert_fusion.2), channel_id=1, source_target_pairs={{0,4},{1,5},{2,6},{3,7},{4,0},{5,1},{6,2},{7,3}} | collective-permute-start | bytes 6291464 | tf_op jit(solution)/shard_map/ppermute | solution.py:33
  1013.8 62.7 %collective-permute-start.24 = (f16[528,2048]{1,0:T(8,128)(2,1)S(1)}, f16[528,2048]{1,0:T(8,128)(2,1)}, u32[]{:S(2)}, u32[]{:S(2)}) collective-permute-start(f16[528,2048]{1,0:T(8,128)(2,1)S(1)} %concatenate.22), channel_id=1, source_target_pairs={{0,4},{1,5},{2,6},{3,7},{4,0},{5,1},{6,2},{7,3}} | collective-permute-start | bytes 6488072 | tf_op jit(solution)/shard_map/ppermute | solution.py:33
  1015.2 61.3 %slice-start.2 = ((s8[8388608]{0:T(1024)(128)(4,1)}), s8[4194304]{0:T(1024)(128)(4,1)S(1)}, s32[]{:S(2)}) async-start(s8[8388608]{0:T(1024)(128)(4,1)} %bitcast.148), calls=%async_computation.10 | async-start | bytes 8388608
  1034.5 76.7 %collective-permute-start.18 = (f16[528,2048]{1,0:T(8,128)(2,1)S(1)}, f16[528,2048]{1,0:T(8,128)(2,1)}, u32[]{:S(2)}, u32[]{:S(2)}) collective-permute-start(f16[528,2048]{1,0:T(8,128)(2,1)S(1)} %concatenate.22), channel_id=1, source_target_pairs={{0,1},{1,0},{2,3},{3,2},{4,5},{5,4},{6,7},{7,6}} | collective-permute-start | bytes 6488072 | tf_op jit(solution)/shard_map/ppermute | solution.py:33
  1039.7 84.8 %collective-permute-start.20 = (f16[528,2048]{1,0:T(8,128)(2,1)S(1)}, f16[528,2048]{1,0:T(8,128)(2,1)}, u32[]{:S(2)}, u32[]{:S(2)}) collective-permute-start(f16[528,2048]{1,0:T(8,128)(2,1)S(1)} %concatenate.22), channel_id=1, source_target_pairs={{0,2},{1,3},{2,0},{3,1},{4,6},{5,7},{6,4},{7,5}} | collective-permute-start | bytes 6488072 | tf_op jit(solution)/shard_map/ppermute | solution.py:33
  1076.5 50.6 %collective-permute-start.25 = (f16[528,2048]{1,0:T(8,128)(2,1)}, f16[528,2048]{1,0:T(8,128)(2,1)}, u32[]{:S(2)}, u32[]{:S(2)}) collective-permute-start(f16[528,2048]{1,0:T(8,128)(2,1)} %collective-permute-done.24), channel_id=1, source_target_pairs={{0,1},{1,0},{2,3},{3,2},{4,5},{5,4},{6,7},{7,6}} | collective-permute-start | bytes 6488072 | tf_op jit(solution)/shard_map/ppermute | solution.py:33
  1120.8 98.3 %collective-permute-start.26 = (f16[528,2048]{1,0:T(8,128)(2,1)S(1)}, f16[528,2048]{1,0:T(8,128)(2,1)}, u32[]{:S(2)}, u32[]{:S(2)}) collective-permute-start(f16[528,2048]{1,0:T(8,128)(2,1)S(1)} %concatenate.23), channel_id=1, source_target_pairs={{0,4},{1,5},{2,6},{3,7},{4,0},{5,1},{6,2},{7,3}} | collective-permute-start | bytes 6488072 | tf_op jit(solution)/shard_map/ppermute | solution.py:33
  1122.1 98.9 %collective-permute-start.22 = (f16[528,2048]{1,0:T(8,128)(2,1)S(1)}, f16[528,2048]{1,0:T(8,128)(2,1)}, u32[]{:S(2)}, u32[]{:S(2)}) collective-permute-start(f16[528,2048]{1,0:T(8,128)(2,1)S(1)} %concatenate.23), channel_id=1, source_target_pairs={{0,2},{1,3},{2,0},{3,1},{4,6},{5,7},{6,4},{7,5}} | collective-permute-start | bytes 6488072 | tf_op jit(solution)/shard_map/ppermute | solution.py:33
  1122.7 100.2 %collective-permute-start.19 = (f16[528,2048]{1,0:T(8,128)(2,1)S(1)}, f16[528,2048]{1,0:T(8,128)(2,1)}, u32[]{:S(2)}, u32[]{:S(2)}) collective-permute-start(f16[528,2048]{1,0:T(8,128)(2,1)S(1)} %concatenate.23), channel_id=1, source_target_pairs={{0,1},{1,0},{2,3},{3,2},{4,5},{5,4},{6,7},{7,6}} | collective-permute-start | bytes 6488072 | tf_op jit(solution)/shard_map/ppermute | solution.py:33
  1126.5 90.1 %collective-permute-start.28 = (f16[528,2048]{1,0:T(8,128)(2,1)}, f16[528,2048]{1,0:T(8,128)(2,1)S(1)}, u32[]{:S(2)}, u32[]{:S(2)}) collective-permute-start(f16[528,2048]{1,0:T(8,128)(2,1)} %collective-permute-done.20), channel_id=1, source_target_pairs={{0,4},{1,5},{2,6},{3,7},{4,0},{5,1},{6,2},{7,3}} | collective-permute-start | bytes 6488072 | tf_op jit(solution)/shard_map/ppermute | solution.py:33
  1127.1 90.6 %collective-permute-start.21 = (f16[528,2048]{1,0:T(8,128)(2,1)}, f16[528,2048]{1,0:T(8,128)(2,1)S(1)}, u32[]{:S(2)}, u32[]{:S(2)}) collective-permute-start(f16[528,2048]{1,0:T(8,128)(2,1)} %collective-permute-done.20), channel_id=1, source_target_pairs={{0,1},{1,0},{2,3},{3,2},{4,5},{5,4},{6,7},{7,6}} | collective-permute-start | bytes 6488072 | tf_op jit(solution)/shard_map/ppermute | solution.py:33
  1224.9 15.9 %collective-permute-start.29 = (f16[528,2048]{1,0:T(8,128)(2,1)S(1)}, f16[528,2048]{1,0:T(8,128)(2,1)S(1)}, u32[]{:S(2)}, u32[]{:S(2)}) collective-permute-start(f16[528,2048]{1,0:T(8,128)(2,1)S(1)} %collective-permute-done.28), channel_id=1, source_target_pairs={{0,1},{1,0},{2,3},{3,2},{4,5},{5,4},{6,7},{7,6}} | collective-permute-start | bytes 6488072 | tf_op jit(solution)/shard_map/ppermute | solution.py:33
  1224.9 49.6 %collective-permute-start.30 = (f16[528,2048]{1,0:T(8,128)(2,1)}, f16[528,2048]{1,0:T(8,128)(2,1)S(1)}, u32[]{:S(2)}, u32[]{:S(2)}) collective-permute-start(f16[528,2048]{1,0:T(8,128)(2,1)} %collective-permute-done.26), channel_id=1, source_target_pairs={{0,2},{1,3},{2,0},{3,1},{4,6},{5,7},{6,4},{7,5}} | collective-permute-start | bytes 6488072 | tf_op jit(solution)/shard_map/ppermute | solution.py:33
  1225.5 50.4 %collective-permute-start.27 = (f16[528,2048]{1,0:T(8,128)(2,1)}, f16[528,2048]{1,0:T(8,128)(2,1)S(1)}, u32[]{:S(2)}, u32[]{:S(2)}) collective-permute-start(f16[528,2048]{1,0:T(8,128)(2,1)} %collective-permute-done.26), channel_id=1, source_target_pairs={{0,1},{1,0},{2,3},{3,2},{4,5},{5,4},{6,7},{7,6}} | collective-permute-start | bytes 6488072 | tf_op jit(solution)/shard_map/ppermute | solution.py:33
  1225.7 51.4 %collective-permute-start.23 = (f16[528,2048]{1,0:T(8,128)(2,1)}, f16[528,2048]{1,0:T(8,128)(2,1)S(1)}, u32[]{:S(2)}, u32[]{:S(2)}) collective-permute-start(f16[528,2048]{1,0:T(8,128)(2,1)} %collective-permute-done.22), channel_id=1, source_target_pairs={{0,1},{1,0},{2,3},{3,2},{4,5},{5,4},{6,7},{7,6}} | collective-permute-start | bytes 6488072 | tf_op jit(solution)/shard_map/ppermute | solution.py:33
  1278.4 24.8 %collective-permute-start.31 = (f16[528,2048]{1,0:T(8,128)(2,1)S(1)}, f16[528,2048]{1,0:T(8,128)(2,1)S(1)}, u32[]{:S(2)}, u32[]{:S(2)}) collective-permute-start(f16[528,2048]{1,0:T(8,128)(2,1)S(1)} %collective-permute-done.30), channel_id=1, source_target_pairs={{0,1},{1,0},{2,3},{3,2},{4,5},{5,4},{6,7},{7,6}} | collective-permute-start | bytes 6488072 | tf_op jit(solution)/shard_map/ppermute | solution.py:33
  (11 other events, 262.5 us)
Sparse Core Ops, SparseCore 0:
  129.0 30.0 all-gather.10
  160.6 28.4 all-gather.12
  190.6 28.4 all-gather.14
  220.5 28.4 all-gather.8
  333.7 28.7 all-gather.20
  467.0 36.8 all-gather.18
  505.4 28.4 all-gather.22
  586.0 27.3 all-gather.16

commit v2 on v1

--- a/solution.py
+++ b/solution.py
@@ -3,6 +3,7 @@
 import jax.numpy as jnp
 from jax import lax
 from jax.experimental import pallas as pl
+from jax.experimental.pallas import tpu as pltpu
 from jax.sharding import PartitionSpec as P
 
 
@@ -10,11 +11,16 @@
 PRECISE = lax.Precision.HIGHEST
 HALF_TOP = 32768.0
 WIRE = jnp.float16
+GELU_C, GELU_A = (2.0 / 3.141592653589793) ** 0.5, 0.044715
+PARTS, SLOTS = 4, 8
 
 
 def gelu_grad(pre_act, d_act):
-    pullback = jax.vjp(functools.partial(jax.nn.gelu, approximate=True), pre_act.astype(jnp.float32))[1]
-    return pullback(d_act.astype(jnp.float32))[0].astype(jnp.bfloat16)
+    z = pre_act.astype(jnp.float32)
+    cubic = (GELU_C * GELU_A) * (z * z)
+    tanh = jnp.tanh(z * (cubic + GELU_C))
+    slope = 3.0 * cubic + GELU_C
+    return (d_act.astype(jnp.float32) * (0.5 + 0.5 * (tanh + z * (slope - tanh * tanh * slope)))).astype(jnp.bfloat16)
 
 
 def cross_rows(left_op, right_op):
@@ -69,10 +75,56 @@
             return cross_rows(lhs, right)
 
         def chosen(vals, rels):
-            def branch(k, vals):
-                return tuple(vals[k ^ rel] for rel in rels)
-
-            return lax.switch(chip, [functools.partial(branch, k) for k in range(n_layers)], vals)
+            rows = vals[0].shape[0] // PARTS
+            work = [(rel, out, part) for out, rel in enumerate(rels) for part in range(PARTS)]
+
+            def kernel(*refs):
+                ins, outs = refs[:n_layers], refs[n_layers:n_layers + len(rels)]
+                buf, in_sem, out_sem = refs[n_layers + len(rels):]
+                here = lax.axis_index("data") // 2
+
+                def fetch(n):
+                    rel, _, part = work[n]
+                    slot = n % SLOTS
+                    for k in range(n_layers):
+                        @pl.when(here == k)
+                        def _():
+                            src = ins[k ^ rel].at[pl.ds(part * rows, rows)]
+                            pltpu.make_async_copy(src, buf.at[slot], in_sem.at[slot]).start()
+
+                def leave(n):
+                    _, out, part = work[n]
+                    slot = n % SLOTS
+                    return pltpu.make_async_copy(buf.at[slot], outs[out].at[pl.ds(part * rows, rows)], out_sem.at[slot])
+
+                ahead = SLOTS // 2
+                for n in range(len(work) + ahead):
+                    if n < len(work):
+                        if n >= SLOTS:
+                            leave(n - SLOTS).wait()
+                        fetch(n)
+                    if n >= ahead:
+                        slot = (n - ahead) % SLOTS
+                        pltpu.make_async_copy(ins[0].at[pl.ds(0, rows)], buf.at[slot], in_sem.at[slot]).wait()
+                        leave(n - ahead).start()
+                for n in range(max(len(work) - SLOTS, 0), len(work)):
+                    leave(n).wait()
+
+            shape = jax.ShapeDtypeStruct(vals[0].shape, vals[0].dtype)
+            any_spec = pl.BlockSpec(memory_space=pl.ANY)
+            size = vals[0].size * 2
+            return pl.pallas_call(
+                kernel,
+                out_shape=(shape,) * len(rels),
+                in_specs=[any_spec] * n_layers,
+                out_specs=(any_spec,) * len(rels),
+                scratch_shapes=[
+                    pltpu.VMEM((SLOTS, rows, vals[0].shape[1]), vals[0].dtype),
+                    pltpu.SemaphoreType.DMA((SLOTS,)),
+                    pltpu.SemaphoreType.DMA((SLOTS,)),
+                ],
+                cost_estimate=pl.CostEstimate(flops=size * len(rels) * 8, bytes_accessed=2 * size * len(rels), transcendentals=0),
+            )(*vals)
 
         def gathered(vals, rels):
             return {rel: pair_rows(val) for rel, val in zip(rels, lax.optimization_barrier(vals))}
@@ -94,11 +146,13 @@
                 self.mid_x, self.mid_y = hop(sent_x, 2), hop(sent_y, 4)
                 return sent_y
 
-            def direct(self, *done):
+            def direct(self, *done, between=None):
                 sent_x = partial_sum(self.operands, self.scales, 1, 0, half, (), done)
-                sent_y = partial_sum(self.operands, self.scales, 2, half, half, (), (sent_x,))
-                self.near_x, self.near_y = hop(sent_x, 2), hop(sent_y, 4)
-                return sent_y
+                self.near_x = hop(sent_x, 2)
+                filled = between(sent_x) if between else sent_x
+                sent_y = partial_sum(self.operands, self.scales, 2, half, half, (), (filled,))
+                self.near_y = hop(sent_y, 4)
+                return sent_y, filled
 
             def joined(self, *done):
                 sent_y = partial_sum(self.operands, self.scales, 2, 0, half, (self.mid_x,), done)
@@ -131,13 +185,16 @@
         h_top = jnp.append(h_top, 1.1 * h_top[2] * w3_norm)
         pre_3, act_3, _ = forward(act_2, weights[2])
         order = (3, 1, 2, 0)
-        h_rot = gathered(chosen((x_loc, act_1, act_2, act_3), order), order)
+        h_vals = (x_loc, act_1, act_2, act_3)
+        first_h = chosen(h_vals, (3,))
+        h_rot = gathered(first_h, (3,))
         routes_a = Routes((h_rot, h_rot), scale_of(h_top, h_top))
 
         g_peaks = [peak(dy_loc)]
         grad_3, top = backward(after(dy_loc, act_3), weights[3], pre_3)
         g_peaks.append(top)
         done, mid = routes_a.whole(3, 2, (), grad_3)
+        h_rot.update(gathered(chosen(after(h_vals, done), order[1:]), order[1:]))
         grad_2, top = backward(after(grad_3, done), weights[2], pre_2)
         g_peaks.append(top)
         g_top = everywhere(jnp.stack(g_peaks[::-1]))
@@ -153,11 +210,10 @@
         routes_g = Routes((h_rot, g_rot), scale_of(h_top, g_top))
         routes_s = Routes((g_rot, g_rot), scale_of(g_top, g_top))
         done = routes_g.opposite(done)
-        done = routes_g.direct(done)
-        a_new = routes_a.final(a_old_rows, done)
-        done = routes_g.joined(a_new)
+        done, a_new = routes_g.direct(done, between=functools.partial(routes_a.final, a_old_rows))
+        done = routes_g.joined(done)
         done = routes_s.opposite(done)
-        done = routes_s.direct(done)
+        done, _ = routes_s.direct(done)
         g_sum = routes_g.final(None, done)
         s_inv_own = lax.dynamic_index_in_dim(s_inv, chip, axis=0, keepdims=False)
         right = jnp.dot(g_sum, s_inv_own, precision=PRECISE)
@@ -180,8 +236,8 @@
         )()
 
         def place(u_full, part, rel, which, first):
-            power = part[half, 0].astype(jnp.float32)
-            val = (part[:half].astype(jnp.float32) * jnp.exp2(power - 15.0))[None]
+            back = jnp.exp2(part[half:half + 1].astype(jnp.float32) - 15.0)
+            val = (part[:half].astype(jnp.float32) * back)[None]
             return lax.dynamic_update_slice(u_full, val, (chip ^ rel, which * own + first, 0))
 
         coded, prev = [], done

time: 1320 us -> 1270 us (0.962)
  local copies, waits for them, and re-layouts: 76.4 us -> 3.1 us
  Pallas kernels: 0.01 us -> 49.5 us
  waiting for transfers between devices: 400 us -> 383 us
    cond x7 -> x0, local copies, waits for them, and re-layouts: 58.4 us -> none
    pallas_call x0 -> x4, Pallas kernels: none -> 49.5 us  [chosen(): pl.pallas_call(kernel, out_shape=(shape,) * len(rels), in_specs=[any_spec...]
    ppermute x36, waiting for transfers between devices: 398 us -> 381 us  [hop(): return lax.ppermute(val, 'data', [(p, p ^ mask) for p in range(n_dev)])]
  transfers between devices with their start and end apart: 44 -> 44, of which waited for: 13 -> 18; matrix products, arithmetic and copies ran while one was open for 48% -> 52% of each run, Pallas kernels for 0% -> 2%
where the time goes in v2:
time: 1270 us; the launch traced here: 1260 us
  matrix products  651 us (51%)
  waiting for transfers between devices  383 us (30%)
  other arithmetic  111 us (9%)
  Pallas kernels  49.5 us (4%)
  starting transfers between devices  36.2 us (3%)
  between operations  30.2 us (2%)
    ppermute x36, waiting for transfers between devices, hop(): return lax.ppermute(val, 'data', [(p, p ^ mask) for p in range(n_dev)])  381 us
    dot_general x18, matrix products, cross_rows(): jnp.einsum('bi,bj->ij', left_op, right_op, preferred_element_type=jnp.flo...  319 us
    dot_general x3, matrix products, backward(): jnp.einsum('bj,ij->bi', grad, weight, preferred_element_type=jnp.float32)  106 us
    dot_general x3, matrix products, forward(): jnp.dot(act, weight, preferred_element_type=jnp.float32)  87.2 us
    dot_general x1, matrix products, device_step(): right = jnp.dot(g_sum, s_inv_own, precision=PRECISE)  68.9 us
    dynamic_update_slice x16, other arithmetic, place(): lax.dynamic_update_slice(u_full, val, (chip ^ rel, which * own + first, 0))  54.9 us
    pallas_call x4, Pallas kernels, chosen(): pl.pallas_call(kernel, out_shape=(shape,) * len(rels), in_specs=[any_spec...  49.5 us
    dot_general x2, matrix products, device_step(): jnp.dot(inv_other, after(right_other, u_piece), precision=PRECISE)  35.9 us
  transfers between devices with their start and end apart: 44, of which 18 were waited for; matrix products, arithmetic and copies ran while one was open for 52% of the time, Pallas kernels for 2%

profile of v2, /device:TPU:0, one launch (start us, length us, event | category | flops | bytes accessed | tf_op | source)
XLA Modules:
  0.0 1263.9 jit_solution(6826204046609657789)
XLA Ops:
  7.2 29.4 %abs_reduce_fusion.7 = (bf16[]{:T(256)}, bf16[2048,2048]{1,0:T(8,128)(2,1)}, bf16[2048,2048]{1,0:T(8,128)(2,1)}) fusion(bf16[2048,2048]{1,0:T(8,128)(2,1)} %refs_0_.2, bf16[4,2048,2048]{2,1,0:T(8,128)(2,1)} %param.9), kind=kOutput, calls=%fused_computation.113 | convolution fusion | flops 17234395136 | bytes 33554432 | tf_op jit(solution)/shard_map/dot_general | solution.py:64
  37.2 29.5 %abs_reduce_fusion.6 = (bf16[]{:T(256)}, bf16[2048,2048]{1,0:T(8,128)(2,1)}, bf16[2048,2048]{1,0:T(8,128)(2,1)}) fusion(bf16[2048,2048]{1,0:T(8,128)(2,1)} %get-tuple-element.64.refs_1_, bf16[4,2048,2048]{2,1,0:T(8,128)(2,1)} %param.9), kind=kOutput, calls=%fused_computation.112 | convolution fusion | flops 17234395136 | bytes 33554432 | tf_op jit(solution)/shard_map/dot_general | solution.py:64
  67.4 28.3 %fusion.47 = (bf16[2048,2048]{1,0:T(8,128)(2,1)}, bf16[2048,2048]{1,0:T(8,128)(2,1)}) fusion(bf16[2048,2048]{1,0:T(8,128)(2,1)} %get-tuple-element.65.refs_2_, bf16[4,2048,2048]{2,1,0:T(8,128)(2,1)} %param.9), kind=kOutput, calls=%fused_computation.71 | convolution fusion | flops 17226006528 | bytes 33554432 | tf_op jit(solution)/shard_map/dot_general | solution.py:64
  95.7 7.0 shard_map.95
  102.8 6.0 abs_reduce_fusion.5
  110.4 36.3 %abs_reduce_fusion.4 = (bf16[]{:T(256)}, bf16[2048,2048]{1,0:T(8,128)(2,1)}) fusion(bf16[2048,2048]{1,0:T(8,128)(2,1)} %get-tuple-element.60, bf16[2048,2048]{1,0:T(8,128)(2,1)} %refs_3_.2, bf16[4,2048,2048]{2,1,0:T(8,128)(2,1)} %param.9), kind=kOutput, calls=%fused_computation.107 | convolution fusion | flops 17263755264 | bytes 33554432 | tf_op jit(solution)/shard_map/bj,ij->bi/dot_general | solution.py:69
  147.4 8.2 abs_reduce_fusion
  167.3 23.9 %multiply_convert_fusion.1 = f16[1024,2048]{1,0:T(8,128)(2,1)} fusion(f32[]{:T(128)} %bitcast.8, bf16[4096,2048]{1,0:T(8,128)(2,1)} %all-gather.9.cloned.1.call-done, s32[]{:T(128)S(6)} %select_n.29), kind=kOutput, calls=%fused_computation.106 | convolution fusion | flops 17184063488 | bytes 29360644 | tf_op jit(solution)/shard_map/bi,bj->ij/dot_general | solution.py:27
  191.2 17.7 %shard_map.96 = (bf16[2048,2048]{1,0:T(8,128)(2,1)}, bf16[2048,2048]{1,0:T(8,128)(2,1)}, bf16[2048,2048]{1,0:T(8,128)(2,1)}) custom-call(bf16[2048,2048]{1,0:T(8,128)(2,1)} %refs_0_.2, bf16[2048,2048]{1,0:T(8,128)(2,1)} %get-tuple-element.64.refs_1_, bf16[2048,2048]{1,0:T(8,128)(2,1)} %get-tuple-element.65.refs_2_, bf16[2048,2048]{1,0:T(8,128)(2,1)} %get-tuple-element.66.refs_3_), custom_call_target="tpu_custom_call" | custom-call | flops 201326592 | bytes 50331648 | tf_op jit(solution)/shard_map/pallas_call | solution.py:116
  210.9 35.3 %abs_reduce_fusion.3 = (bf16[]{:T(256)}, bf16[2048,2048]{1,0:T(8,128)(2,1)}) fusion(bf16[2048,2048]{1,0:T(8,128)(2,1)} %get-tuple-element.69, bf16[2048,2048]{1,0:T(8,128)(2,1)} %get-tuple-element.79.refs_2_, bf16[4,2048,2048]{2,1,0:T(8,128)(2,1)} %param.9), kind=kOutput, calls=%fused_computation.105 | convolution fusion | flops 17263755264 | bytes 33554432 | tf_op jit(solution)/shard_map/bj,ij->bi/dot_general | solution.py:69
  246.9 26.8 %multiply_convert_fusion = f16[1024,2048]{1,0:T(8,128)(2,1)} fusion(f32[]{:T(128)} %bitcast.10, bf16[4096,2048]{1,0:T(8,128)(2,1)} %all-gather.13.cloned.1.call-done, s32[]{:T(128)S(6)} %select_n.29), kind=kOutput, calls=%fused_computation.102 | convolution fusion | flops 17184063488 | bytes 29360644 | tf_op jit(solution)/shard_map/bi,bj->ij/dot_general | solution.py:27
  273.7 34.9 %fusion.29.refs_0_ = bf16[2048,2048]{1,0:T(8,128)(2,1)} fusion(bf16[2048,2048]{1,0:T(8,128)(2,1)} %get-tuple-element.74, bf16[2048,2048]{1,0:T(8,128)(2,1)} %get-tuple-element.78.refs_1_, bf16[4,2048,2048]{2,1,0:T(8,128)(2,1)} %param.9), kind=kOutput, calls=%fused_computation.53 | convolution fusion | flops 17255366656 | bytes 33554432 | tf_op jit(solution)/shard_map/bj,ij->bi/dot_general | solution.py:69
  308.5 7.0 shard_map.97
  318.4 85.0 %collective-permute-done.3 = f16[1024,2048]{1,0:T(8,128)(2,1)} collective-permute-done((f16[1024,2048]{1,0:T(8,128)(2,1)}, f16[1024,2048]{1,0:T(8,128)(2,1)}, u32[]{:S(2)}, u32[]{:S(2)}) %collective-permute-start.3) | collective-permute-done | bytes 4194336 | tf_op jit(solution)/shard_map/ppermute | solution.py:39
  403.4 24.4 %add_convert_fusion = f16[1024,2048]{1,0:T(8,128)(2,1)} fusion(f16[1024,2048]{1,0:T(8,128)(2,1)} %collective-permute-done.3, f32[]{:T(128)} %bitcast.11, bf16[4096,2048]{1,0:T(8,128)(2,1)} %all-gather.15.cloned.1.call-done, s32[]{:T(128)S(6)} %select_n.29), kind=kOutput, calls=%fused_computation.99 | convolution fusion | flops 17188257792 | bytes 33554948 | tf_op jit(solution)/shard_map/bi,bj->ij/dot_general | solution.py:27
  427.8 17.8 %shard_map.98 = (bf16[2048,2048]{1,0:T(8,128)(2,1)}, bf16[2048,2048]{1,0:T(8,128)(2,1)}, bf16[2048,2048]{1,0:T(8,128)(2,1)}) custom-call(bf16[2048,2048]{1,0:T(8,128)(2,1)} %fusion.29.refs_0_, bf16[2048,2048]{1,0:T(8,128)(2,1)} %get-tuple-element.78.refs_1_, bf16[2048,2048]{1,0:T(8,128)(2,1)} %get-tuple-element.79.refs_2_, bf16[2048,2048]{1,0:T(8,128)(2,1)} %refs_3_.2), custom_call_target="tpu_custom_call" | custom-call | flops 201326592 | bytes 50331648 | tf_op jit(solution)/shard_map/pallas_call | solution.py:116
  446.6 5.9 abs_reduce_fusion.2
  472.3 24.1 %fusion.92 = f32[1024,2048]{1,0:T(8,128)} fusion(bf16[4096,2048]{1,0:T(8,128)(2,1)} %all-gather.11.cloned.1.call-done, s32[]{:T(128)S(6)} %select_n.29), kind=kOutput, calls=%fused_computation.118 | convolution fusion | flops 17179869184 | bytes 33554436 | tf_op jit(solution)/shard_map/bi,bj->ij/dot_general | solution.py:27
  496.4 14.8 %multiply_convert_fusion.11 = f16[512,2048]{1,0:T(8,128)(2,1)} fusion(bf16[4096,2048]{1,0:T(8,128)(2,1)} %all-gather.21.cloned.1.call-done, bf16[4096,2048]{1,0:T(8,128)(2,1)} %all-gather.9.cloned.1.call-done, s32[]{:T(128)S(6)} %select_n.29, f32[]{:T(128)} %bitcast.18), kind=kOutput, calls=%fused_computation.179 | convolution fusion | flops 8592031744 | bytes 23069188 | tf_op jit(solution)/shard_map/bi,bj->ij/dot_general | solution.py:27
  512.4 12.4 multiply_convert_fusion.10
  526.0 14.8 %multiply_convert_fusion.9 = f16[512,2048]{1,0:T(8,128)(2,1)} fusion(bf16[4096,2048]{1,0:T(8,128)(2,1)} %all-gather.19.cloned.1.call-done, bf16[4096,2048]{1,0:T(8,128)(2,1)} %all-gather.13.cloned.1.call-done, s32[]{:T(128)S(6)} %select_n.29, f32[]{:T(128)} %bitcast.17), kind=kOutput, calls=%fused_computation.177 | convolution fusion | flops 8592031744 | bytes 23069188 | tf_op jit(solution)/shard_map/bi,bj->ij/dot_general | solution.py:27
  541.9 20.8 %collective-permute-done.8 = f16[1024,2048]{1,0:T(8,128)(2,1)} collective-permute-done((f16[1024,2048]{1,0:T(8,128)(2,1)}, f16[1024,2048]{1,0:T(8,128)(2,1)}, u32[]{:S(2)}, u32[]{:S(2)}) %collective-permute-start.8) | collective-permute-done | bytes 4194336 | tf_op jit(solution)/shard_map/ppermute | solution.py:39
  564.4 13.5 %multiply_add_fusion = f32[1024,2048]{1,0:T(8,128)} fusion(f16[1024,2048]{1,0:T(8,128)(2,1)} %collective-permute-done.9, f16[1024,2048]{1,0:T(8,128)(2,1)} %collective-permute-done.8, f32[1024,2048]{1,0:T(8,128)} %fusion.92, f32[1024,2048]{1,0:T(8,128)} %param.10, f32[]{:T(128)} %bitcast.20), kind=kLoop, calls=%fused_computation.97 | loop fusion | flops 18874368 | bytes 33554436 | tf_op jit(solution)/shard_map/add | solution.py:174
  577.9 14.8 %multiply_convert_fusion.8 = f16[512,2048]{1,0:T(8,128)(2,1)} fusion(bf16[4096,2048]{1,0:T(8,128)(2,1)} %all-gather.23.cloned.1.call-done, bf16[4096,2048]{1,0:T(8,128)(2,1)} %all-gather.15.cloned.1.call-done, s32[]{:T(128)S(6)} %select_n.34, f32[]{:T(128)} %bitcast.19), kind=kOutput, calls=%fused_computation.172 | convolution fusion | flops 8592031744 | bytes 23069188 | tf_op jit(solution)/shard_map/bi,bj->ij/dot_general | solution.py:27
  594.2 13.4 %collective-permute-done.10 = f16[512,2048]{1,0:T(8,128)(2,1)} collective-permute-done((f16[512,2048]{1,0:T(8,128)(2,1)}, f16[512,2048]{1,0:T(8,128)(2,1)}, u32[]{:S(2)}, u32[]{:S(2)}) %collective-permute-start.10) | collective-permute-done | bytes 2097184 | tf_op jit(solution)/shard_map/ppermute | solution.py:39
  607.6 15.0 %add_convert_fusion.4 = f16[512,2048]{1,0:T(8,128)(2,1)} fusion(f16[512,2048]{1,0:T(8,128)(2,1)} %collective-permute-done.10, bf16[4096,2048]{1,0:T(8,128)(2,1)} %all-gather.23.cloned.1.call-done, bf16[4096,2048]{1,0:T(8,128)(2,1)} %all-gather.15.cloned.1.call-done, s32[]{:T(128)S(6)} %select_n.29, f32[]{:T(128)} %bitcast.19), kind=kOutput, calls=%fused_computation.171 | convolution fusion | flops 8594128896 | bytes 25166340 | tf_op jit(solution)/shard_map/bi,bj->ij/dot_general | solution.py:27
  622.7 12.6 add_convert_fusion.3
  635.3 14.7 %multiply_convert_fusion.7 = f16[512,2048]{1,0:T(8,128)(2,1)} fusion(bf16[4096,2048]{1,0:T(8,128)(2,1)} %all-gather.21.cloned.1.call-done, s32[]{:T(128)S(6)} %select_n.29, f32[]{:T(128)} %bitcast.24), kind=kOutput, calls=%fused_computation.157 | convolution fusion | flops 8592031744 | bytes 23069188 | tf_op jit(solution)/shard_map/bi,bj->ij/dot_general | solution.py:27
  653.7 14.6 %multiply_convert_fusion.6 = f16[512,2048]{1,0:T(8,128)(2,1)} fusion(bf16[4096,2048]{1,0:T(8,128)(2,1)} %all-gather.21.cloned.1.call-done, s32[]{:T(128)S(6)} %select_n.34, f32[]{:T(128)} %bitcast.24), kind=kOutput, calls=%fused_computation.156 | convolution fusion | flops 8592031744 | bytes 23069188 | tf_op jit(solution)/shard_map/bi,bj->ij/dot_general | solution.py:27
  668.4 14.8 %multiply_convert_fusion.5 = f16[512,2048]{1,0:T(8,128)(2,1)} fusion(bf16[4096,2048]{1,0:T(8,128)(2,1)} %all-gather.19.cloned.1.call-done, s32[]{:T(128)S(6)} %select_n.29, f32[]{:T(128)} %bitcast.23), kind=kOutput, calls=%fused_computation.155 | convolution fusion | flops 8592031744 | bytes 23069188 | tf_op jit(solution)/shard_map/bi,bj->ij/dot_general | solution.py:27
  683.2 14.6 %multiply_convert_fusion.4 = f16[512,2048]{1,0:T(8,128)(2,1)} fusion(bf16[4096,2048]{1,0:T(8,128)(2,1)} %all-gather.23.cloned.1.call-done, s32[]{:T(128)S(6)} %select_n.34, f32[]{:T(128)} %bitcast.22), kind=kOutput, calls=%fused_computation.154 | convolution fusion | flops 8592031744 | bytes 23069188 | tf_op jit(solution)/shard_map/bi,bj->ij/dot_general | solution.py:27
  700.7 38.6 %collective-permute-done.14 = f16[512,2048]{1,0:T(8,128)(2,1)S(1)} collective-permute-done((f16[512,2048]{1,0:T(8,128)(2,1)S(1)}, f16[512,2048]{1,0:T(8,128)(2,1)S(1)}, u32[]{:S(2)}, u32[]{:S(2)}) %collective-permute-start.14) | collective-permute-done | bytes 2097184 | tf_op jit(solution)/shard_map/ppermute | solution.py:39
  742.1 24.8 %fusion.51 = f32[1024,2048]{1,0:T(8,128)} fusion(f32[512,2048]{1,0:T(8,128)} %convert_add_fusion.5, f32[512,2048]{1,0:T(8,128)} %convert_add_fusion.6, f32[]{:T(128)} %bitcast.21, bf16[4096,2048]{1,0:T(8,128)(2,1)} %all-gather.17.cloned.1.call-done, bf16[4096,2048]{1,0:T(8,128)(2,1)} %all-gather.11.cloned.1.call-done, s32[]{:T(128)S(6)} %select_n.29), kind=kOutput, calls=%fused_computation.78 | convolution fusion | flops 17188257792 | bytes 41943556 | tf_op jit(solution)/shard_map/bi,bj->ij/dot_general | solution.py:27
  766.9 68.9 %fusion.48 = f32[1024,2048]{1,0:T(8,128)} fusion(f32[1024,2048]{1,0:T(8,128)} %fusion.51, f32[4,2048,2048]{2,1,0:T(8,128)} %param.13, s32[]{:T(128)S(6)} %select_n.36), kind=kOutput, calls=%fused_computation.72 | convolution fusion | flops 51539607552 | bytes 33554436 | tf_op jit(solution)/shard_map/dot_general | solution.py:219
  837.9 15.0 %add_convert_fusion.2 = f16[512,2048]{1,0:T(8,128)(2,1)} fusion(f16[512,2048]{1,0:T(8,128)(2,1)} %collective-permute-done.15, bf16[4096,2048]{1,0:T(8,128)(2,1)} %all-gather.23.cloned.1.call-done, s32[]{:T(128)S(6)} %select_n.29, f32[]{:T(128)} %bitcast.22), kind=kOutput, calls=%fused_computation.149 | convolution fusion | flops 8594128896 | bytes 25166340 | tf_op jit(solution)/shard_map/bi,bj->ij/dot_general | solution.py:27
  852.9 31.5 %collective-permute-done.16 = f16[512,2048]{1,0:T(8,128)(2,1)} collective-permute-done((f16[512,2048]{1,0:T(8,128)(2,1)S(1)}, f16[512,2048]{1,0:T(8,128)(2,1)}, u32[]{:S(2)}, u32[]{:S(2)}) %collective-permute-start.16) | collective-permute-done | bytes 2097184 | tf_op jit(solution)/shard_map/ppermute | solution.py:39
  884.5 11.5 add_convert_fusion.1
  900.4 17.1 %fusion.162 = f32[512,2048]{1,0:T(8,128)S(1)} fusion(f32[1024,2048]{1,0:T(8,128)} %fusion.48, f32[1024,2048]{1,0:T(8,128)} %param.12, s32[]{:T(128)S(6)} %select_n.29), kind=kOutput, calls=%fused_computation.192 | convolution fusion | flops 12884901888 | bytes 14680068 | tf_op jit(solution)/shard_map/dot_general | solution.py:247
  917.5 11.7 collective-permute-done.34
  929.3 15.5 %collective-permute-done.35 = f16[512,2048]{1,0:T(8,128)(2,1)} collective-permute-done((f16[512,2048]{1,0:T(8,128)(2,1)}, f16[512,2048]{1,0:T(8,128)(2,1)}, u32[]{:S(2)}, u32[]{:S(2)}) %collective-permute-start.35) | collective-permute-done | bytes 2097184 | tf_op jit(solution)/shard_map/ppermute | solution.py:39
  949.2 18.2 %abs_reduce_fusion.9 = (f32[]{:T(128)}, f32[512,2048]{1,0:T(8,128)}) fusion(f32[512,2048]{1,0:T(8,128)S(1)} %fusion.162, f32[1024,2048]{1,0:T(8,128)} %collective-permute-done.17, f32[1024,2048]{1,0:T(8,128)} %param.12, s32[]{:T(128)S(6)} %select_n.37), kind=kOutput, calls=%fused_computation.147 | convolution fusion | flops 12888047616 | bytes 18874376 | tf_op jit(solution)/shard_map/dot_general | solution.py:248
  974.2 13.7 %collective-permute-done.32 = f16[512,2048]{1,0:T(8,128)(2,1)} collective-permute-done((f16[512,2048]{1,0:T(8,128)(2,1)}, f16[512,2048]{1,0:T(8,128)(2,1)}, u32[]{:S(2)}, u32[]{:S(2)}) %collective-permute-start.32) | collective-permute-done | bytes 2097184 | tf_op jit(solution)/shard_map/ppermute | solution.py:39
  994.7 16.1 %fusion.159 = f32[512,2048]{1,0:T(8,128)S(1)} fusion(f32[1024,2048]{1,0:T(8,128)} %fusion.48, f32[1024,2048]{1,0:T(8,128)S(1)} %bitcast.147, s32[]{:T(128)S(6)} %select_n.29), kind=kOutput, calls=%fused_computation.189 | convolution fusion | flops 12884901888 | bytes 14680068 | tf_op jit(solution)/shard_map/dot_general | solution.py:247
  1010.8 17.7 %abs_reduce_fusion.8 = (f32[]{:T(128)}, f32[512,2048]{1,0:T(8,128)}) fusion(f32[512,2048]{1,0:T(8,128)S(1)} %fusion.159, f32[1024,2048]{1,0:T(8,128)} %collective-permute-done.17, f32[1024,2048]{1,0:T(8,128)S(1)} %bitcast.147, s32[]{:T(128)S(6)} %select_n.37), kind=kOutput, calls=%fused_computation.145 | convolution fusion | flops 12888047616 | bytes 18874376 | tf_op jit(solution)/shard_map/dot_general | solution.py:248
  1042.4 25.6 %fusion.54 = f32[1024,2048]{1,0:T(8,128)} fusion(f32[512,2048]{1,0:T(8,128)S(1)} %copy-done.1, f32[512,2048]{1,0:T(8,128)S(1)} %copy-done.2, f32[1024,2048]{1,0:T(8,128)} %param.11, f32[]{:T(128)} %bitcast.56, bf16[4096,2048]{1,0:T(8,128)(2,1)} %all-gather.17.cloned.1.call-done, s32[]{:T(128)S(6)} %select_n.29), kind=kOutput, calls=%fused_computation.82 | convolution fusion | flops 17194549248 | bytes 50332164 | tf_op jit(solution)/shard_map/bi,bj->ij/dot_general | solution.py:27
  1068.0 11.2 collective-permute-done.24
  1080.8 88.2 %collective-permute-done.28 = f16[528,2048]{1,0:T(8,128)(2,1)} collective-permute-done((f16[528,2048]{1,0:T(8,128)(2,1)}, f16[528,2048]{1,0:T(8,128)(2,1)}, u32[]{:S(2)}, u32[]{:S(2)}) %collective-permute-start.28) | collective-permute-done | bytes 2162720 | tf_op jit(solution)/shard_map/ppermute | solution.py:39
  1188.5 40.8 %collective-permute-done.30 = f16[528,2048]{1,0:T(8,128)(2,1)S(1)} collective-permute-done((f16[528,2048]{1,0:T(8,128)(2,1)}, f16[528,2048]{1,0:T(8,128)(2,1)S(1)}, u32[]{:S(2)}, u32[]{:S(2)}) %collective-permute-start.30) | collective-permute-done | bytes 2162720 | tf_op jit(solution)/shard_map/ppermute | solution.py:39
  (180 shorter events, 129.4 us)
Async XLA Ops:
  7.2 160.1 %all-gather.9.cloned.1.call-start = ((), (), s32[]{:S(2)}) async-start(), calls=%async_computation | async-start | bytes 25165824 | tf_op jit(solution)/shard_map/all_gather | solution.py:42
  102.8 144.1 %all-gather.13.cloned.1.call-start = ((), (), s32[]{:S(2)}) async-start(), calls=%async_computation.2 | async-start | bytes 25165824 | tf_op jit(solution)/shard_map/all_gather | solution.py:42
  109.6 46.7 %collective-permute-start = (f32[3]{0:T(128)S(1)}, f32[3]{0:T(128)S(1)}, u32[]{:S(2)}, u32[]{:S(2)}) collective-permute-start(f32[3]{0:T(128)S(1)} %pad_maximum_fusion), channel_id=1, source_target_pairs={{0,1},{1,0},{2,3},{3,2},{4,5},{5,4},{6,7},{7,6}} | collective-permute-start | bytes 44 | tf_op jit(solution)/shard_map/ppermute | solution.py:39
  156.4 3.9 collective-permute-start.1
  160.4 3.6 collective-permute-start.2
  208.9 194.5 %all-gather.15.cloned.1.call-start = ((), (), s32[]{:S(2)}) async-start(), calls=%async_computation.3 | async-start | bytes 25165824 | tf_op jit(solution)/shard_map/all_gather | solution.py:42
  209.7 262.6 %all-gather.11.cloned.1.call-start = ((), (), s32[]{:S(2)}) async-start(), calls=%async_computation.1 | async-start | bytes 25165824 | tf_op jit(solution)/shard_map/all_gather | solution.py:42
  210.2 286.2 %all-gather.21.cloned.1.call-start = ((), (), s32[]{:S(2)}) async-start(), calls=%async_computation.6 | async-start | bytes 25165824 | tf_op jit(solution)/shard_map/all_gather | solution.py:42
  315.6 210.4 %all-gather.19.cloned.1.call-start = ((), (), s32[]{:S(2)}) async-start(), calls=%async_computation.5 | async-start | bytes 25165824 | tf_op jit(solution)/shard_map/all_gather | solution.py:42
  315.6 87.7 %collective-permute-start.3 = (f16[1024,2048]{1,0:T(8,128)(2,1)}, f16[1024,2048]{1,0:T(8,128)(2,1)}, u32[]{:S(2)}, u32[]{:S(2)}) collective-permute-start(f16[1024,2048]{1,0:T(8,128)(2,1)} %multiply_convert_fusion.1), channel_id=1, source_target_pairs={{0,2},{1,3},{2,0},{3,1},{4,6},{5,7},{6,4},{7,5}} | collective-permute-start | bytes 12582920 | tf_op jit(solution)/shard_map/ppermute | solution.py:39
  445.6 132.3 %all-gather.23.cloned.1.call-start = ((), (), s32[]{:S(2)}) async-start(), calls=%async_computation.7 | async-start | bytes 25165824 | tf_op jit(solution)/shard_map/all_gather | solution.py:42
  446.3 295.8 %all-gather.17.cloned.1.call-start = ((), (), s32[]{:S(2)}) async-start(), calls=%async_computation.4 | async-start | bytes 25165824 | tf_op jit(solution)/shard_map/all_gather | solution.py:42
  454.5 1.2 collective-permute-start.4
  455.8 3.6 collective-permute-start.5
  459.4 3.6 collective-permute-start.6
  468.9 93.8 %collective-permute-start.8 = (f16[1024,2048]{1,0:T(8,128)(2,1)}, f16[1024,2048]{1,0:T(8,128)(2,1)}, u32[]{:S(2)}, u32[]{:S(2)}) collective-permute-start(f16[1024,2048]{1,0:T(8,128)(2,1)} %multiply_convert_fusion), channel_id=1, source_target_pairs={{0,2},{1,3},{2,0},{3,1},{4,6},{5,7},{6,4},{7,5}} | collective-permute-start | bytes 12582920 | tf_op jit(solution)/shard_map/ppermute | solution.py:39
  470.7 93.8 %collective-permute-start.9 = (f16[1024,2048]{1,0:T(8,128)(2,1)}, f16[1024,2048]{1,0:T(8,128)(2,1)}, u32[]{:S(2)}, u32[]{:S(2)}) collective-permute-start(f16[1024,2048]{1,0:T(8,128)(2,1)} %add_convert_fusion), channel_id=1, source_target_pairs={{0,4},{1,5},{2,6},{3,7},{4,0},{5,1},{6,2},{7,3}} | collective-permute-start | bytes 12582920 | tf_op jit(solution)/shard_map/ppermute | solution.py:39
  511.2 96.4 %collective-permute-start.10 = (f16[512,2048]{1,0:T(8,128)(2,1)}, f16[512,2048]{1,0:T(8,128)(2,1)}, u32[]{:S(2)}, u32[]{:S(2)}) collective-permute-start(f16[512,2048]{1,0:T(8,128)(2,1)} %multiply_convert_fusion.11), channel_id=1, source_target_pairs={{0,2},{1,3},{2,0},{3,1},{4,6},{5,7},{6,4},{7,5}} | collective-permute-start | bytes 6291464 | tf_op jit(solution)/shard_map/ppermute | solution.py:39
  524.8 97.9 %collective-permute-start.13 = (f16[512,2048]{1,0:T(8,128)(2,1)}, f16[512,2048]{1,0:T(8,128)(2,1)}, u32[]{:S(2)}, u32[]{:S(2)}) collective-permute-start(f16[512,2048]{1,0:T(8,128)(2,1)} %multiply_convert_fusion.10), channel_id=1, source_target_pairs={{0,4},{1,5},{2,6},{3,7},{4,0},{5,1},{6,2},{7,3}} | collective-permute-start | bytes 6291464 | tf_op jit(solution)/shard_map/ppermute | solution.py:39
  540.9 157.0 %collective-permute-start.7 = (f16[512,2048]{1,0:T(8,128)(2,1)}, f16[512,2048]{1,0:T(8,128)(2,1)S(1)}, u32[]{:S(2)}, u32[]{:S(2)}) collective-permute-start(f16[512,2048]{1,0:T(8,128)(2,1)} %multiply_convert_fusion.9), channel_id=1, source_target_pairs={{0,2},{1,3},{2,0},{3,1},{4,6},{5,7},{6,4},{7,5}} | collective-permute-start | bytes 6291464 | tf_op jit(solution)/shard_map/ppermute | solution.py:39
  592.7 108.0 %collective-permute-start.12 = (f16[512,2048]{1,0:T(8,128)(2,1)}, f16[512,2048]{1,0:T(8,128)(2,1)S(1)}, u32[]{:S(2)}, u32[]{:S(2)}) collective-permute-start(f16[512,2048]{1,0:T(8,128)(2,1)} %multiply_convert_fusion.8), channel_id=1, source_target_pairs={{0,4},{1,5},{2,6},{3,7},{4,0},{5,1},{6,2},{7,3}} | collective-permute-start | bytes 6291464 | tf_op jit(solution)/shard_map/ppermute | solution.py:39
  650.0 187.9 %collective-permute-start.15 = (f16[512,2048]{1,0:T(8,128)(2,1)}, f16[512,2048]{1,0:T(8,128)(2,1)}, u32[]{:S(2)}, u32[]{:S(2)}) collective-permute-start(f16[512,2048]{1,0:T(8,128)(2,1)} %multiply_convert_fusion.7), channel_id=1, source_target_pairs={{0,2},{1,3},{2,0},{3,1},{4,6},{5,7},{6,4},{7,5}} | collective-permute-start | bytes 6291464 | tf_op jit(solution)/shard_map/ppermute | solution.py:39
  651.7 87.5 %collective-permute-start.14 = (f16[512,2048]{1,0:T(8,128)(2,1)S(1)}, f16[512,2048]{1,0:T(8,128)(2,1)S(1)}, u32[]{:S(2)}, u32[]{:S(2)}) collective-permute-start(f16[512,2048]{1,0:T(8,128)(2,1)S(1)} %copy-done.8), channel_id=1, source_target_pairs={{0,2},{1,3},{2,0},{3,1},{4,6},{5,7},{6,4},{7,5}} | collective-permute-start | bytes 6291464 | tf_op jit(solution)/shard_map/ppermute | solution.py:39
  652.0 45.8 %collective-permute-start.11 = (f16[512,2048]{1,0:T(8,128)(2,1)S(1)}, f16[512,2048]{1,0:T(8,128)(2,1)S(1)}, u32[]{:S(2)}, u32[]{:S(2)}) collective-permute-start(f16[512,2048]{1,0:T(8,128)(2,1)S(1)} %copy-done.9), channel_id=1, source_target_pairs={{0,4},{1,5},{2,6},{3,7},{4,0},{5,1},{6,2},{7,3}} | collective-permute-start | bytes 6291464 | tf_op jit(solution)/shard_map/ppermute | solution.py:39
  766.9 68.9 %copy-start.7 = (f16[512,2048]{1,0:T(8,128)(2,1)S(1)}, f16[512,2048]{1,0:T(8,128)(2,1)}, u32[]{:S(2)}) copy-start(f16[512,2048]{1,0:T(8,128)(2,1)} %multiply_convert_fusion.6) | copy-start | bytes 6291460
  766.9 117.5 %slice-start.6 = ((s8[16777216]{0:T(1024)(128)(4,1)}), s8[4194304]{0:T(1024)(128)(4,1)S(1)}, s32[]{:S(2)}) async-start(s8[16777216]{0:T(1024)(128)(4,1)} %bitcast.165), calls=%async_computation.14 | async-start | bytes 8388608
  766.9 117.5 %slice-start.7 = ((s8[16777216]{0:T(1024)(128)(4,1)}), s8[4194304]{0:T(1024)(128)(4,1)S(1)}, s32[]{:S(2)}) async-start(s8[16777216]{0:T(1024)(128)(4,1)} %bitcast.165), calls=%async_computation.15 | async-start | bytes 8388608
  766.9 117.5 %slice-start.8 = ((s8[16777216]{0:T(1024)(128)(4,1)}), s8[4194304]{0:T(1024)(128)(4,1)S(1)}, s32[]{:S(2)}) async-start(s8[16777216]{0:T(1024)(128)(4,1)} %bitcast.165), calls=%async_computation.16 | async-start | bytes 8388608
  835.8 113.4 %collective-permute-start.17 = (f32[1024,2048]{1,0:T(8,128)}, f32[1024,2048]{1,0:T(8,128)}, u32[]{:S(2)}, u32[]{:S(2)}) collective-permute-start(f32[1024,2048]{1,0:T(8,128)} %fusion.48), channel_id=1, source_target_pairs={{0,1},{1,0},{2,3},{3,2},{4,5},{5,4},{6,7},{7,6}} | collective-permute-start | bytes 25165832 | tf_op jit(solution)/shard_map/ppermute | solution.py:39
  835.8 48.6 %collective-permute-start.16 = (f16[512,2048]{1,0:T(8,128)(2,1)S(1)}, f16[512,2048]{1,0:T(8,128)(2,1)}, u32[]{:S(2)}, u32[]{:S(2)}) collective-permute-start(f16[512,2048]{1,0:T(8,128)(2,1)S(1)} %copy-done.7), channel_id=1, source_target_pairs={{0,4},{1,5},{2,6},{3,7},{4,0},{5,1},{6,2},{7,3}} | collective-permute-start | bytes 6291464 | tf_op jit(solution)/shard_map/ppermute | solution.py:39
  837.6 91.7 %collective-permute-start.34 = (f16[512,2048]{1,0:T(8,128)(2,1)}, f16[512,2048]{1,0:T(8,128)(2,1)S(1)}, u32[]{:S(2)}, u32[]{:S(2)}) collective-permute-start(f16[512,2048]{1,0:T(8,128)(2,1)} %multiply_convert_fusion.4), channel_id=1, source_target_pairs={{0,4},{1,5},{2,6},{3,7},{4,0},{5,1},{6,2},{7,3}} | collective-permute-start | bytes 6291464 | tf_op jit(solution)/shard_map/ppermute | solution.py:39
  895.9 48.8 %collective-permute-start.35 = (f16[512,2048]{1,0:T(8,128)(2,1)}, f16[512,2048]{1,0:T(8,128)(2,1)}, u32[]{:S(2)}, u32[]{:S(2)}) collective-permute-start(f16[512,2048]{1,0:T(8,128)(2,1)} %add_convert_fusion.1), channel_id=1, source_target_pairs={{0,2},{1,3},{2,0},{3,1},{4,6},{5,7},{6,4},{7,5}} | collective-permute-start | bytes 6291464 | tf_op jit(solution)/shard_map/ppermute | solution.py:39
  898.3 89.6 %collective-permute-start.32 = (f16[512,2048]{1,0:T(8,128)(2,1)}, f16[512,2048]{1,0:T(8,128)(2,1)}, u32[]{:S(2)}, u32[]{:S(2)}) collective-permute-start(f16[512,2048]{1,0:T(8,128)(2,1)} %multiply_convert_fusion.5), channel_id=1, source_target_pairs={{0,2},{1,3},{2,0},{3,1},{4,6},{5,7},{6,4},{7,5}} | collective-permute-start | bytes 6291464 | tf_op jit(solution)/shard_map/ppermute | solution.py:39
  898.7 89.3 %collective-permute-start.33 = (f16[512,2048]{1,0:T(8,128)(2,1)}, f16[512,2048]{1,0:T(8,128)(2,1)}, u32[]{:S(2)}, u32[]{:S(2)}) collective-permute-start(f16[512,2048]{1,0:T(8,128)(2,1)} %add_convert_fusion.2), channel_id=1, source_target_pairs={{0,4},{1,5},{2,6},{3,7},{4,0},{5,1},{6,2},{7,3}} | collective-permute-start | bytes 6291464 | tf_op jit(solution)/shard_map/ppermute | solution.py:39
  974.2 56.7 %collective-permute-start.18 = (f16[528,2048]{1,0:T(8,128)(2,1)S(1)}, f16[528,2048]{1,0:T(8,128)(2,1)}, u32[]{:S(2)}, u32[]{:S(2)}) collective-permute-start(f16[528,2048]{1,0:T(8,128)(2,1)S(1)} %concatenate.22), channel_id=1, source_target_pairs={{0,1},{1,0},{2,3},{3,2},{4,5},{5,4},{6,7},{7,6}} | collective-permute-start | bytes 6488072 | tf_op jit(solution)/shard_map/ppermute | solution.py:39
  993.0 47.9 %collective-permute-start.20 = (f16[528,2048]{1,0:T(8,128)(2,1)S(1)}, f16[528,2048]{1,0:T(8,128)(2,1)}, u32[]{:S(2)}, u32[]{:S(2)}) collective-permute-start(f16[528,2048]{1,0:T(8,128)(2,1)S(1)} %concatenate.22), channel_id=1, source_target_pairs={{0,2},{1,3},{2,0},{3,1},{4,6},{5,7},{6,4},{7,5}} | collective-permute-start | bytes 6488072 | tf_op jit(solution)/shard_map/ppermute | solution.py:39
  1029.2 50.0 %collective-permute-start.24 = (f16[528,2048]{1,0:T(8,128)(2,1)S(1)}, f16[528,2048]{1,0:T(8,128)(2,1)}, u32[]{:S(2)}, u32[]{:S(2)}) collective-permute-start(f16[528,2048]{1,0:T(8,128)(2,1)S(1)} %concatenate.22), channel_id=1, source_target_pairs={{0,4},{1,5},{2,6},{3,7},{4,0},{5,1},{6,2},{7,3}} | collective-permute-start | bytes 6488072 | tf_op jit(solution)/shard_map/ppermute | solution.py:39
  1039.6 139.7 %collective-permute-start.26 = (f16[528,2048]{1,0:T(8,128)(2,1)S(1)}, f16[528,2048]{1,0:T(8,128)(2,1)}, u32[]{:S(2)}, u32[]{:S(2)}) collective-permute-start(f16[528,2048]{1,0:T(8,128)(2,1)S(1)} %concatenate.23), channel_id=1, source_target_pairs={{0,4},{1,5},{2,6},{3,7},{4,0},{5,1},{6,2},{7,3}} | collective-permute-start | bytes 6488072 | tf_op jit(solution)/shard_map/ppermute | solution.py:39
  1040.1 140.4 %collective-permute-start.22 = (f16[528,2048]{1,0:T(8,128)(2,1)S(1)}, f16[528,2048]{1,0:T(8,128)(2,1)}, u32[]{:S(2)}, u32[]{:S(2)}) collective-permute-start(f16[528,2048]{1,0:T(8,128)(2,1)S(1)} %concatenate.23), channel_id=1, source_target_pairs={{0,2},{1,3},{2,0},{3,1},{4,6},{5,7},{6,4},{7,5}} | collective-permute-start | bytes 6488072 | tf_op jit(solution)/shard_map/ppermute | solution.py:39
  1040.4 129.3 %collective-permute-start.19 = (f16[528,2048]{1,0:T(8,128)(2,1)S(1)}, f16[528,2048]{1,0:T(8,128)(2,1)}, u32[]{:S(2)}, u32[]{:S(2)}) collective-permute-start(f16[528,2048]{1,0:T(8,128)(2,1)S(1)} %concatenate.23), channel_id=1, source_target_pairs={{0,1},{1,0},{2,3},{3,2},{4,5},{5,4},{6,7},{7,6}} | collective-permute-start | bytes 6488072 | tf_op jit(solution)/shard_map/ppermute | solution.py:39
  1040.9 128.1 %collective-permute-start.28 = (f16[528,2048]{1,0:T(8,128)(2,1)}, f16[528,2048]{1,0:T(8,128)(2,1)}, u32[]{:S(2)}, u32[]{:S(2)}) collective-permute-start(f16[528,2048]{1,0:T(8,128)(2,1)} %collective-permute-done.20), channel_id=1, source_target_pairs={{0,4},{1,5},{2,6},{3,7},{4,0},{5,1},{6,2},{7,3}} | collective-permute-start | bytes 6488072 | tf_op jit(solution)/shard_map/ppermute | solution.py:39
  1079.2 109.2 %collective-permute-start.25 = (f16[528,2048]{1,0:T(8,128)(2,1)}, f16[528,2048]{1,0:T(8,128)(2,1)S(1)}, u32[]{:S(2)}, u32[]{:S(2)}) collective-permute-start(f16[528,2048]{1,0:T(8,128)(2,1)} %collective-permute-done.24), channel_id=1, source_target_pairs={{0,1},{1,0},{2,3},{3,2},{4,5},{5,4},{6,7},{7,6}} | collective-permute-start | bytes 6488072 | tf_op jit(solution)/shard_map/ppermute | solution.py:39
  1168.9 12.3 collective-permute-start.21
  1169.7 75.4 %collective-permute-start.29 = (f16[528,2048]{1,0:T(8,128)(2,1)}, f16[528,2048]{1,0:T(8,128)(2,1)S(1)}, u32[]{:S(2)}, u32[]{:S(2)}) collective-permute-start(f16[528,2048]{1,0:T(8,128)(2,1)} %collective-permute-done.28), channel_id=1, source_target_pairs={{0,1},{1,0},{2,3},{3,2},{4,5},{5,4},{6,7},{7,6}} | collective-permute-start | bytes 6488072 | tf_op jit(solution)/shard_map/ppermute | solution.py:39
  1180.0 49.2 %collective-permute-start.30 = (f16[528,2048]{1,0:T(8,128)(2,1)}, f16[528,2048]{1,0:T(8,128)(2,1)S(1)}, u32[]{:S(2)}, u32[]{:S(2)}) collective-permute-start(f16[528,2048]{1,0:T(8,128)(2,1)} %collective-permute-done.26), channel_id=1, source_target_pairs={{0,2},{1,3},{2,0},{3,1},{4,6},{5,7},{6,4},{7,5}} | collective-permute-start | bytes 6488072 | tf_op jit(solution)/shard_map/ppermute | solution.py:39
  1180.5 55.5 %collective-permute-start.27 = (f16[528,2048]{1,0:T(8,128)(2,1)}, f16[528,2048]{1,0:T(8,128)(2,1)S(1)}, u32[]{:S(2)}, u32[]{:S(2)}) collective-permute-start(f16[528,2048]{1,0:T(8,128)(2,1)} %collective-permute-done.26), channel_id=1, source_target_pairs={{0,1},{1,0},{2,3},{3,2},{4,5},{5,4},{6,7},{7,6}} | collective-permute-start | bytes 6488072 | tf_op jit(solution)/shard_map/ppermute | solution.py:39
  1181.2 48.0 %collective-permute-start.23 = (f16[528,2048]{1,0:T(8,128)(2,1)}, f16[528,2048]{1,0:T(8,128)(2,1)S(1)}, u32[]{:S(2)}, u32[]{:S(2)}) collective-permute-start(f16[528,2048]{1,0:T(8,128)(2,1)} %collective-permute-done.22), channel_id=1, source_target_pairs={{0,1},{1,0},{2,3},{3,2},{4,5},{5,4},{6,7},{7,6}} | collective-permute-start | bytes 6488072 | tf_op jit(solution)/shard_map/ppermute | solution.py:39
  1229.2 25.0 %collective-permute-start.31 = (f16[528,2048]{1,0:T(8,128)(2,1)S(1)}, f16[528,2048]{1,0:T(8,128)(2,1)S(1)}, u32[]{:S(2)}, u32[]{:S(2)}) collective-permute-start(f16[528,2048]{1,0:T(8,128)(2,1)S(1)} %collective-permute-done.30), channel_id=1, source_target_pairs={{0,1},{1,0},{2,3},{3,2},{4,5},{5,4},{6,7},{7,6}} | collective-permute-start | bytes 6488072 | tf_op jit(solution)/shard_map/ppermute | solution.py:39
  (16 other events, 380.2 us)
Sparse Core Ops, SparseCore 0:
  102.9 30.0 all-gather.8
  209.0 28.7 all-gather.12
  239.4 28.4 all-gather.14
  269.2 28.4 all-gather.10
  315.7 28.8 all-gather.20
  445.7 28.5 all-gather.18
  475.8 28.4 all-gather.22
  505.8 28.4 all-gather.16

commit v3 on v2

--- a/solution.py
+++ b/solution.py
@@ -1,4 +1,3 @@
-import functools
 import jax
 import jax.numpy as jnp
 from jax import lax
@@ -12,7 +11,7 @@
 HALF_TOP = 32768.0
 WIRE = jnp.float16
 GELU_C, GELU_A = (2.0 / 3.141592653589793) ** 0.5, 0.044715
-PARTS, SLOTS = 4, 8
+PARTS, SLOTS = 8, 16
 
 
 def gelu_grad(pre_act, d_act):
@@ -70,9 +69,9 @@
             grad = gelu_grad(pre, d_act)
             return lax.optimization_barrier((grad, peak(grad)))
 
-        def product(left, right, first, rows):
-            lhs = lax.dynamic_slice(left, (0, core * own + first), (left.shape[0], rows))
-            return cross_rows(lhs, right)
+        def product(left, right, first, cols):
+            lhs = lax.dynamic_slice(left, (0, core * own), (left.shape[0], own))
+            return cross_rows(lhs, right[:, first:first + cols])
 
         def chosen(vals, rels):
             rows = vals[0].shape[0] // PARTS
@@ -129,9 +128,9 @@
         def gathered(vals, rels):
             return {rel: pair_rows(val) for rel, val in zip(rels, lax.optimization_barrier(vals))}
 
-        def partial_sum(operands, scales, rel, first, rows, arrived, done):
+        def partial_sum(operands, scales, rel, first, cols, arrived, done):
             scale = after(scales[chip ^ rel] / batch_total, *done)
-            out = product(operands[0][rel], operands[1][rel], first, rows) * scale
+            out = product(operands[0][rel], operands[1][rel], first, cols) * scale
             for part in arrived:
                 out = out + part.astype(jnp.float32)
             return lax.optimization_barrier(out.astype(WIRE))
@@ -141,35 +140,35 @@
                 self.operands, self.scales = operands, scales
 
             def opposite(self, *done):
-                sent_x = partial_sum(self.operands, self.scales, 3, 0, half, (), done)
-                sent_y = partial_sum(self.operands, self.scales, 3, half, half, (), (sent_x,))
+                sent_x = partial_sum(self.operands, self.scales, 3, 0, own, (), done)
+                sent_y = partial_sum(self.operands, self.scales, 3, own, own, (), (sent_x,))
                 self.mid_x, self.mid_y = hop(sent_x, 2), hop(sent_y, 4)
                 return sent_y
 
             def direct(self, *done, between=None):
-                sent_x = partial_sum(self.operands, self.scales, 1, 0, half, (), done)
+                sent_x = partial_sum(self.operands, self.scales, 1, 0, own, (), done)
                 self.near_x = hop(sent_x, 2)
                 filled = between(sent_x) if between else sent_x
-                sent_y = partial_sum(self.operands, self.scales, 2, half, half, (), (filled,))
+                sent_y = partial_sum(self.operands, self.scales, 2, own, own, (), (filled,))
                 self.near_y = hop(sent_y, 4)
                 return sent_y, filled
 
             def joined(self, *done):
-                sent_y = partial_sum(self.operands, self.scales, 2, 0, half, (self.mid_x,), done)
-                sent_x = partial_sum(self.operands, self.scales, 1, half, half, (self.mid_y,), (sent_y,))
+                sent_y = partial_sum(self.operands, self.scales, 2, 0, own, (self.mid_x,), done)
+                sent_x = partial_sum(self.operands, self.scales, 1, own, own, (self.mid_y,), (sent_y,))
                 far_x, far_y = hop(sent_y, 4), hop(sent_x, 2)
                 self.parts = ((self.near_x, far_x), (self.near_y, far_y))
                 return sent_x
 
             def whole(self, rel, mask, arrived, *done):
-                sent = partial_sum(self.operands, self.scales, rel, 0, own, arrived, done)
+                sent = partial_sum(self.operands, self.scales, rel, 0, width, arrived, done)
                 return sent, hop(sent, mask)
 
             def final(self, old, *done):
                 inv = after(1.0 / self.scales[chip], *done)
                 wire = [near.astype(jnp.float32) + far.astype(jnp.float32) for near, far in self.parts]
-                wire = jnp.concatenate(wire, axis=0) if len(wire) > 1 else wire[0]
-                mean = product(self.operands[0][0], self.operands[1][0], 0, own) / batch_total + wire * inv
+                wire = jnp.concatenate(wire, axis=1) if len(wire) > 1 else wire[0]
+                mean = product(self.operands[0][0], self.operands[1][0], 0, width) / batch_total + wire * inv
                 if old is not None:
                     mean = FACTOR_DECAY * old + (1.0 - FACTOR_DECAY) * mean
                 return lax.optimization_barrier(mean)
@@ -200,17 +199,18 @@
         g_top = everywhere(jnp.stack(g_peaks[::-1]))
         g_top = jnp.concatenate([(1.25 * g_top[0] * w2_norm)[None], g_top])
         done, near = routes_a.whole(1, 2, (), grad_2)
+        done, far = routes_a.whole(2, 4, (mid,), done)
+        routes_a.parts = ((near, far),)
         grad_1, _ = backward(after(grad_2, done), weights[1], pre_1)
         first_rot = chosen((grad_1, grad_2, grad_3, dy_loc), (3,))
         g_rot = gathered(first_rot, (3,))
-        done, far = routes_a.whole(2, 4, (mid,), first_rot[0])
-        routes_a.parts = ((near, far),)
+        done = first_rot[0]
         g_rot.update(gathered(chosen(after((grad_1, grad_2, grad_3, dy_loc), done), order[1:]), order[1:]))
 
         routes_g = Routes((h_rot, g_rot), scale_of(h_top, g_top))
         routes_s = Routes((g_rot, g_rot), scale_of(g_top, g_top))
         done = routes_g.opposite(done)
-        done, a_new = routes_g.direct(done, between=functools.partial(routes_a.final, a_old_rows))
+        done, _ = routes_g.direct(done)
         done = routes_g.joined(done)
         done = routes_s.opposite(done)
         done, _ = routes_s.direct(done)
@@ -252,10 +252,13 @@
         from_y = [hop(part, 4) for part in coded]
         diag = [hop(from_x[0], 4), hop(from_y[1], 2)]
         s_new = routes_s.final(s_old_rows, prev)
+        a_new = routes_a.final(a_old_rows, s_new)
         for parts, rel in ((coded, 0), (from_x, 1), (from_y, 2), (diag, 3)):
+            other = [hop(part, 1) for part in parts]
             for part, first in zip(parts, (0, half)):
                 u_full = place(u_full, part, rel, core, first)
-                u_full = place(u_full, hop(part, 1), rel, 1 - core, first)
+            for part, first in zip(other, (0, half)):
+                u_full = place(u_full, part, rel, 1 - core, first)
         return u_full, a_new, s_new
 
     row_spec = P("data", None)

time: 1270 us -> 1100 us (0.87)
  waiting for transfers between devices: 383 us -> 211 us
    ppermute x36, waiting for transfers between devices: 381 us -> 209 us  [hop(): return lax.ppermute(val, 'data', [(p, p ^ mask) for p in range(n_dev)])]
    dot_general x18, matrix products: 319 us -> 336 us  [cross_rows(): jnp.einsum('bi,bj->ij', left_op, right_op, preferred_element_type=jnp.flo...]
  transfers between devices with their start and end apart: 44 -> 44, of which waited for: 18 -> 12; matrix products, arithmetic and copies ran while one was open for 52% -> 54% of each run, Pallas kernels for 2% -> 2%
where the time goes in v3:
time: 1100 us; the launch traced here: 1090 us
  matrix products  657 us (60%)
  waiting for transfers between devices  211 us (19%)
  other arithmetic  99.9 us (9%)
  Pallas kernels  52.2 us (5%)
  starting transfers between devices  34.6 us (3%)
  between operations  29.9 us (3%)
    dot_general x18, matrix products, cross_rows(): jnp.einsum('bi,bj->ij', left_op, right_op, preferred_element_type=jnp.flo...  336 us
    ppermute x36, waiting for transfers between devices, hop(): return lax.ppermute(val, 'data', [(p, p ^ mask) for p in range(n_dev)])  209 us
    dot_general x3, matrix products, backward(): jnp.einsum('bj,ij->bi', grad, weight, preferred_element_type=jnp.float32)  104 us
    dot_general x3, matrix products, forward(): jnp.dot(act, weight, preferred_element_type=jnp.float32)  87 us
    dot_general x1, matrix products, device_step(): right = jnp.dot(g_sum, s_inv_own, precision=PRECISE)  60 us
    pallas_call x4, Pallas kernels, chosen(): pl.pallas_call(kernel, out_shape=(shape,) * len(rels), in_specs=[any_spec...  52.2 us
    dynamic_update_slice x16, other arithmetic, place(): lax.dynamic_update_slice(u_full, val, (chip ^ rel, which * own + first, 0))  50.6 us
    dot_general x2, matrix products, device_step(): jnp.dot(inv_other, after(right_other, u_piece), precision=PRECISE)  37.2 us
  transfers between devices with their start and end apart: 44, of which 12 were waited for; matrix products, arithmetic and copies ran while one was open for 54% of the time, Pallas kernels for 2%

profile of v3, /device:TPU:0, one launch (start us, length us, event | category | flops | bytes accessed | tf_op | source)
XLA Modules:
  0.0 1090.8 jit_solution(3290422551728142855)
XLA Ops:
  7.2 29.4 %abs_reduce_fusion.7 = (bf16[]{:T(256)}, bf16[2048,2048]{1,0:T(8,128)(2,1)}, bf16[2048,2048]{1,0:T(8,128)(2,1)}) fusion(bf16[2048,2048]{1,0:T(8,128)(2,1)} %refs_0_.2, bf16[4,2048,2048]{2,1,0:T(8,128)(2,1)} %param.9), kind=kOutput, calls=%fused_computation.107 | convolution fusion | flops 17234395136 | bytes 33554432 | tf_op jit(solution)/shard_map/dot_general | solution.py:63
  37.2 29.4 %abs_reduce_fusion.6 = (bf16[]{:T(256)}, bf16[2048,2048]{1,0:T(8,128)(2,1)}, bf16[2048,2048]{1,0:T(8,128)(2,1)}) fusion(bf16[2048,2048]{1,0:T(8,128)(2,1)} %get-tuple-element.64.refs_1_, bf16[4,2048,2048]{2,1,0:T(8,128)(2,1)} %param.9), kind=kOutput, calls=%fused_computation.106 | convolution fusion | flops 17234395136 | bytes 33554432 | tf_op jit(solution)/shard_map/dot_general | solution.py:63
  67.3 28.2 %fusion.47 = (bf16[2048,2048]{1,0:T(8,128)(2,1)}, bf16[2048,2048]{1,0:T(8,128)(2,1)}) fusion(bf16[2048,2048]{1,0:T(8,128)(2,1)} %get-tuple-element.65.refs_2_, bf16[4,2048,2048]{2,1,0:T(8,128)(2,1)} %param.9), kind=kOutput, calls=%fused_computation.71 | convolution fusion | flops 17226006528 | bytes 33554432 | tf_op jit(solution)/shard_map/dot_general | solution.py:63
  95.6 6.6 shard_map.95
  102.3 6.0 abs_reduce_fusion.5
  109.9 36.5 %abs_reduce_fusion.4 = (bf16[]{:T(256)}, bf16[2048,2048]{1,0:T(8,128)(2,1)}) fusion(bf16[2048,2048]{1,0:T(8,128)(2,1)} %get-tuple-element.60, bf16[2048,2048]{1,0:T(8,128)(2,1)} %refs_3_.2, bf16[4,2048,2048]{2,1,0:T(8,128)(2,1)} %param.9), kind=kOutput, calls=%fused_computation.103 | convolution fusion | flops 17263755264 | bytes 33554432 | tf_op jit(solution)/shard_map/bj,ij->bi/dot_general | solution.py:68
  147.0 8.2 abs_reduce_fusion
  166.8 23.8 %multiply_convert_fusion.1 = f16[1024,2048]{1,0:T(8,128)(2,1)} fusion(f32[]{:T(128)} %bitcast.8, bf16[4096,2048]{1,0:T(8,128)(2,1)} %all-gather.9.cloned.1.call-done, s32[]{:T(128)S(6)} %select_n.29), kind=kOutput, calls=%fused_computation.102 | convolution fusion | flops 17184063488 | bytes 29360644 | tf_op jit(solution)/shard_map/bi,bj->ij/dot_general | solution.py:26
  190.6 17.9 %shard_map.96 = (bf16[2048,2048]{1,0:T(8,128)(2,1)}, bf16[2048,2048]{1,0:T(8,128)(2,1)}, bf16[2048,2048]{1,0:T(8,128)(2,1)}) custom-call(bf16[2048,2048]{1,0:T(8,128)(2,1)} %refs_0_.2, bf16[2048,2048]{1,0:T(8,128)(2,1)} %get-tuple-element.64.refs_1_, bf16[2048,2048]{1,0:T(8,128)(2,1)} %get-tuple-element.65.refs_2_, bf16[2048,2048]{1,0:T(8,128)(2,1)} %get-tuple-element.66.refs_3_), custom_call_target="tpu_custom_call" | custom-call | flops 201326592 | bytes 50331648 | tf_op jit(solution)/shard_map/pallas_call | solution.py:115
  212.6 36.9 %abs_reduce_fusion.3 = (bf16[]{:T(256)}, bf16[2048,2048]{1,0:T(8,128)(2,1)}) fusion(bf16[2048,2048]{1,0:T(8,128)(2,1)} %get-tuple-element.69, bf16[2048,2048]{1,0:T(8,128)(2,1)} %get-tuple-element.79.refs_2_, bf16[4,2048,2048]{2,1,0:T(8,128)(2,1)} %param.9), kind=kOutput, calls=%fused_computation.101 | convolution fusion | flops 17263755264 | bytes 33554432 | tf_op jit(solution)/shard_map/bj,ij->bi/dot_general | solution.py:68
  250.2 26.1 %multiply_convert_fusion = f16[1024,2048]{1,0:T(8,128)(2,1)} fusion(f32[]{:T(128)} %bitcast.11, bf16[4096,2048]{1,0:T(8,128)(2,1)} %all-gather.15.cloned.1.call-done, s32[]{:T(128)S(6)} %select_n.29), kind=kOutput, calls=%fused_computation.100 | convolution fusion | flops 17184063488 | bytes 29360644 | tf_op jit(solution)/shard_map/bi,bj->ij/dot_general | solution.py:26
  276.3 25.5 %collective-permute-done.3 = f16[1024,2048]{1,0:T(8,128)(2,1)} collective-permute-done((f16[1024,2048]{1,0:T(8,128)(2,1)}, f16[1024,2048]{1,0:T(8,128)(2,1)}, u32[]{:S(2)}, u32[]{:S(2)}) %collective-permute-start.3) | collective-permute-done | bytes 4194336 | tf_op jit(solution)/shard_map/ppermute | solution.py:38
  301.8 24.6 %add_convert_fusion = f16[1024,2048]{1,0:T(8,128)(2,1)} fusion(f16[1024,2048]{1,0:T(8,128)(2,1)} %collective-permute-done.3, f32[]{:T(128)} %bitcast.10, bf16[4096,2048]{1,0:T(8,128)(2,1)} %all-gather.13.cloned.1.call-done, s32[]{:T(128)S(6)} %select_n.29), kind=kOutput, calls=%fused_computation.99 | convolution fusion | flops 17188257792 | bytes 33554948 | tf_op jit(solution)/shard_map/bi,bj->ij/dot_general | solution.py:26
  326.4 30.8 %fusion.29.refs_0_ = bf16[2048,2048]{1,0:T(8,128)(2,1)} fusion(bf16[2048,2048]{1,0:T(8,128)(2,1)} %get-tuple-element.76, bf16[2048,2048]{1,0:T(8,128)(2,1)} %get-tuple-element.78.refs_1_, bf16[4,2048,2048]{2,1,0:T(8,128)(2,1)} %param.9), kind=kOutput, calls=%fused_computation.53 | convolution fusion | flops 17255366656 | bytes 33554432 | tf_op jit(solution)/shard_map/bj,ij->bi/dot_general | solution.py:68
  357.1 6.6 shard_map.97
  363.8 21.1 %shard_map.98 = (bf16[2048,2048]{1,0:T(8,128)(2,1)}, bf16[2048,2048]{1,0:T(8,128)(2,1)}, bf16[2048,2048]{1,0:T(8,128)(2,1)}) custom-call(bf16[2048,2048]{1,0:T(8,128)(2,1)} %fusion.29.refs_0_, bf16[2048,2048]{1,0:T(8,128)(2,1)} %get-tuple-element.78.refs_1_, bf16[2048,2048]{1,0:T(8,128)(2,1)} %get-tuple-element.79.refs_2_, bf16[2048,2048]{1,0:T(8,128)(2,1)} %refs_3_.2), custom_call_target="tpu_custom_call" | custom-call | flops 201326592 | bytes 50331648 | tf_op jit(solution)/shard_map/pallas_call | solution.py:115
  386.8 5.9 abs_reduce_fusion.2
  409.8 17.4 %multiply_convert_fusion.11 = f16[1024,1024]{1,0:T(8,128)(2,1)} fusion(bf16[4096,2048]{1,0:T(8,128)(2,1)} %all-gather.21.cloned.1.call-done, bf16[4096,2048]{1,0:T(8,128)(2,1)} %all-gather.9.cloned.1.call-done, s32[]{:T(128)S(6)} %select_n.29, f32[]{:T(128)} %bitcast.18), kind=kOutput, calls=%fused_computation.197 | convolution fusion | flops 8592031744 | bytes 18874884 | tf_op jit(solution)/shard_map/bi,bj->ij/dot_general | solution.py:26
  429.0 13.7 %multiply_convert_fusion.10 = f16[1024,1024]{1,0:T(8,128)(2,1)} fusion(bf16[4096,2048]{1,0:T(8,128)(2,1)S(1)} %copy-done.8, bf16[4096,2048]{1,0:T(8,128)(2,1)} %all-gather.9.cloned.1.call-done, s32[]{:T(128)S(6)} %select_n.29, f32[]{:T(128)} %bitcast.18), kind=kOutput, calls=%fused_computation.196 | convolution fusion | flops 8592031744 | bytes 18874884 | tf_op jit(solution)/shard_map/bi,bj->ij/dot_general | solution.py:26
  442.7 15.4 %multiply_convert_fusion.9 = f16[1024,1024]{1,0:T(8,128)(2,1)} fusion(bf16[4096,2048]{1,0:T(8,128)(2,1)} %all-gather.19.cloned.1.call-done, bf16[4096,2048]{1,0:T(8,128)(2,1)} %all-gather.15.cloned.1.call-done, s32[]{:T(128)S(6)} %select_n.29, f32[]{:T(128)} %bitcast.17), kind=kOutput, calls=%fused_computation.195 | convolution fusion | flops 8592031744 | bytes 18874884 | tf_op jit(solution)/shard_map/bi,bj->ij/dot_general | solution.py:26
  458.1 18.7 %multiply_convert_fusion.8 = f16[1024,1024]{1,0:T(8,128)(2,1)} fusion(bf16[4096,2048]{1,0:T(8,128)(2,1)} %all-gather.23.cloned.1.call-done, bf16[4096,2048]{1,0:T(8,128)(2,1)} %all-gather.13.cloned.1.call-done, s32[]{:T(128)S(6)} %select_n.29, f32[]{:T(128)} %bitcast.19), kind=kOutput, calls=%fused_computation.194 | convolution fusion | flops 8592031744 | bytes 18874884 | tf_op jit(solution)/shard_map/bi,bj->ij/dot_general | solution.py:26
  480.4 12.6 %add_convert_fusion.4 = f16[1024,1024]{1,0:T(8,128)(2,1)} fusion(f16[1024,1024]{1,0:T(8,128)(2,1)} %collective-permute-done.8, bf16[4096,2048]{1,0:T(8,128)(2,1)S(1)} %copy-done.7, bf16[4096,2048]{1,0:T(8,128)(2,1)} %all-gather.13.cloned.1.call-done, s32[]{:T(128)S(6)} %select_n.29, f32[]{:T(128)} %bitcast.19), kind=kOutput, calls=%fused_computation.193 | convolution fusion | flops 8594128896 | bytes 20972036 | tf_op jit(solution)/shard_map/bi,bj->ij/dot_general | solution.py:26
  494.5 76.0 %collective-permute-done.11 = f16[1024,1024]{1,0:T(8,128)(2,1)} collective-permute-done((f16[1024,1024]{1,0:T(8,128)(2,1)}, f16[1024,1024]{1,0:T(8,128)(2,1)}, u32[]{:S(2)}, u32[]{:S(2)}) %collective-permute-start.11) | collective-permute-done | bytes 2097184 | tf_op jit(solution)/shard_map/ppermute | solution.py:38
  570.5 14.2 %add_convert_fusion.3 = f16[1024,1024]{1,0:T(8,128)(2,1)S(1)} fusion(f16[1024,1024]{1,0:T(8,128)(2,1)} %collective-permute-done.11, bf16[4096,2048]{1,0:T(8,128)(2,1)} %all-gather.19.cloned.1.call-done, bf16[4096,2048]{1,0:T(8,128)(2,1)} %all-gather.15.cloned.1.call-done, s32[]{:T(128)S(6)} %select_n.29, f32[]{:T(128)} %bitcast.17), kind=kOutput, calls=%fused_computation.191 | convolution fusion | flops 8594128896 | bytes 20972036 | tf_op jit(solution)/shard_map/bi,bj->ij/dot_general | solution.py:26
  586.3 15.0 %multiply_convert_fusion.7 = f16[1024,1024]{1,0:T(8,128)(2,1)} fusion(bf16[4096,2048]{1,0:T(8,128)(2,1)} %all-gather.21.cloned.1.call-done, s32[]{:T(128)S(6)} %select_n.29, f32[]{:T(128)} %bitcast.23), kind=kOutput, calls=%fused_computation.189 | convolution fusion | flops 8592031744 | bytes 18874376 | tf_op jit(solution)/shard_map/bi,bj->ij/dot_general | solution.py:26
  601.3 14.8 %multiply_convert_fusion.6 = f16[1024,1024]{1,0:T(8,128)(2,1)} fusion(bf16[4096,2048]{1,0:T(8,128)(2,1)} %all-gather.21.cloned.1.call-done, s32[]{:T(128)S(6)} %select_n.29, f32[]{:T(128)} %bitcast.23), kind=kOutput, calls=%fused_computation.188 | convolution fusion | flops 8592031744 | bytes 18874376 | tf_op jit(solution)/shard_map/bi,bj->ij/dot_general | solution.py:26
  616.1 14.8 %multiply_convert_fusion.5 = f16[1024,1024]{1,0:T(8,128)(2,1)} fusion(bf16[4096,2048]{1,0:T(8,128)(2,1)} %all-gather.19.cloned.1.call-done, s32[]{:T(128)S(6)} %select_n.29, f32[]{:T(128)} %bitcast.22), kind=kOutput, calls=%fused_computation.187 | convolution fusion | flops 8592031744 | bytes 18874376 | tf_op jit(solution)/shard_map/bi,bj->ij/dot_general | solution.py:26
  630.9 15.2 %multiply_convert_fusion.4 = f16[1024,1024]{1,0:T(8,128)(2,1)} fusion(bf16[4096,2048]{1,0:T(8,128)(2,1)} %all-gather.23.cloned.1.call-done, s32[]{:T(128)S(6)} %select_n.29, f32[]{:T(128)} %bitcast.21), kind=kOutput, calls=%fused_computation.186 | convolution fusion | flops 8592031744 | bytes 18874376 | tf_op jit(solution)/shard_map/bi,bj->ij/dot_general | solution.py:26
  656.1 25.1 %fusion.51 = f32[1024,2048]{1,0:T(8,128)} fusion(f32[1024,1024]{1,0:T(8,128)} %convert_add_fusion.5, f32[1024,1024]{1,0:T(8,128)} %convert_add_fusion.6, f32[]{:T(128)} %bitcast.20, bf16[4096,2048]{1,0:T(8,128)(2,1)} %all-gather.17.cloned.1.call-done, bf16[4096,2048]{1,0:T(8,128)(2,1)} %all-gather.11.cloned.1.call-done, s32[]{:T(128)S(6)} %select_n.29), kind=kOutput, calls=%fused_computation.78 | convolution fusion | flops 17188257792 | bytes 41943556 | tf_op jit(solution)/shard_map/bi,bj->ij/dot_general | solution.py:26
  681.2 60.0 %fusion.48 = f32[1024,2048]{1,0:T(8,128)S(1)} fusion(f32[1024,2048]{1,0:T(8,128)} %fusion.51, f32[4,2048,2048]{2,1,0:T(8,128)} %param.13, s32[]{:T(128)S(6)} %select_n.35), kind=kOutput, calls=%fused_computation.72 | convolution fusion | flops 51539607552 | bytes 33554436 | tf_op jit(solution)/shard_map/dot_general | solution.py:219
  741.3 18.2 %add_convert_fusion.2 = f16[1024,1024]{1,0:T(8,128)(2,1)} fusion(f16[1024,1024]{1,0:T(8,128)(2,1)} %collective-permute-done.13, bf16[4096,2048]{1,0:T(8,128)(2,1)} %all-gather.23.cloned.1.call-done, s32[]{:T(128)S(6)} %select_n.29, f32[]{:T(128)} %bitcast.21), kind=kOutput, calls=%fused_computation.185 | convolution fusion | flops 8594128896 | bytes 20971528 | tf_op jit(solution)/shard_map/bi,bj->ij/dot_general | solution.py:26
  760.9 15.1 %add_convert_fusion.1 = f16[1024,1024]{1,0:T(8,128)(2,1)} fusion(f16[1024,1024]{1,0:T(8,128)(2,1)} %collective-permute-done.14, bf16[4096,2048]{1,0:T(8,128)(2,1)} %all-gather.19.cloned.1.call-done, s32[]{:T(128)S(6)} %select_n.29, f32[]{:T(128)} %bitcast.22), kind=kOutput, calls=%fused_computation.184 | convolution fusion | flops 8594128896 | bytes 20971528 | tf_op jit(solution)/shard_map/bi,bj->ij/dot_general | solution.py:26
  776.9 24.6 %fusion.116 = f32[1024,2048]{1,0:T(8,128)} fusion(bf16[4096,2048]{1,0:T(8,128)(2,1)} %all-gather.11.cloned.1.call-done, s32[]{:T(128)S(6)} %select_n.29), kind=kOutput, calls=%fused_computation.142 | convolution fusion | flops 17179869184 | bytes 33554436 | tf_op jit(solution)/shard_map/bi,bj->ij/dot_general | solution.py:26
  801.6 15.6 %fusion.198 = f32[512,2048]{1,0:T(8,128)S(1)} fusion(f32[1024,2048]{1,0:T(8,128)S(1)} %fusion.48, f32[1024,2048]{1,0:T(8,128)} %param.12, s32[]{:T(128)S(6)} %select_n.29), kind=kOutput, calls=%fused_computation.204 | convolution fusion | flops 12884901888 | bytes 14680068 | tf_op jit(solution)/shard_map/dot_general | solution.py:247
  818.4 6.4 collective-permute-done.35
  825.3 4.5 convert_add_fusion.3
  829.9 4.6 convert_add_fusion.4
  834.4 19.0 %abs_reduce_fusion.9 = (f32[]{:T(128)}, f32[512,2048]{1,0:T(8,128)}) fusion(f32[512,2048]{1,0:T(8,128)S(1)} %fusion.198, f32[1024,2048]{1,0:T(8,128)S(1)} %collective-permute-done.15, f32[1024,2048]{1,0:T(8,128)} %param.12, s32[]{:T(128)S(6)} %select_n.36), kind=kOutput, calls=%fused_computation.183 | convolution fusion | flops 12888047616 | bytes 18874376 | tf_op jit(solution)/shard_map/dot_general | solution.py:248
  854.2 5.2 bitcast_dynamic-update-slice_fusion.15
  861.5 16.9 %fusion.195 = f32[512,2048]{1,0:T(8,128)S(1)} fusion(f32[1024,2048]{1,0:T(8,128)} %copy-done.1, f32[1024,2048]{1,0:T(8,128)} %param.12, s32[]{:T(128)S(6)} %select_n.29), kind=kOutput, calls=%fused_computation.201 | convolution fusion | flops 12884901888 | bytes 14680068 | tf_op jit(solution)/shard_map/dot_general | solution.py:247
  878.3 18.3 %abs_reduce_fusion.8 = (f32[]{:T(128)}, f32[512,2048]{1,0:T(8,128)}) fusion(f32[512,2048]{1,0:T(8,128)S(1)} %fusion.195, f32[1024,2048]{1,0:T(8,128)S(1)} %bitcast.135, f32[1024,2048]{1,0:T(8,128)} %param.12, s32[]{:T(128)S(6)} %select_n.36), kind=kOutput, calls=%fused_computation.181 | convolution fusion | flops 12888047616 | bytes 18874376 | tf_op jit(solution)/shard_map/dot_general | solution.py:248
  897.4 5.4 bitcast_dynamic-update-slice_fusion.14
  907.0 26.8 %fusion.54 = f32[1024,2048]{1,0:T(8,128)} fusion(f32[1024,1024]{1,0:T(8,128)S(1)} %copy-done.2, f32[1024,1024]{1,0:T(8,128)} %convert_add_fusion.4, f32[1024,2048]{1,0:T(8,128)} %param.11, f32[]{:T(128)} %bitcast.56, bf16[4096,2048]{1,0:T(8,128)(2,1)} %all-gather.17.cloned.1.call-done, s32[]{:T(128)S(6)} %select_n.29), kind=kOutput, calls=%fused_computation.82 | convolution fusion | flops 17194549248 | bytes 50332164 | tf_op jit(solution)/shard_map/bi,bj->ij/dot_general | solution.py:26
  935.5 9.7 multiply_add_fusion
  945.2 16.8 %collective-permute-done.23 = f16[528,2048]{1,0:T(8,128)(2,1)} collective-permute-done((f16[528,2048]{1,0:T(8,128)(2,1)}, f16[528,2048]{1,0:T(8,128)(2,1)}, u32[]{:S(2)}, u32[]{:S(2)}) %collective-permute-start.23) | collective-permute-done | bytes 2162720 | tf_op jit(solution)/shard_map/ppermute | solution.py:38
  967.9 39.4 %collective-permute-done.18 = f16[528,2048]{1,0:T(8,128)(2,1)S(1)} collective-permute-done((f16[528,2048]{1,0:T(8,128)(2,1)}, f16[528,2048]{1,0:T(8,128)(2,1)S(1)}, u32[]{:S(2)}, u32[]{:S(2)}) %collective-permute-start.18) | collective-permute-done | bytes 2162720 | tf_op jit(solution)/shard_map/ppermute | solution.py:38
  1015.1 34.8 %collective-permute-done.27 = f16[528,2048]{1,0:T(8,128)(2,1)S(1)} collective-permute-done((f16[528,2048]{1,0:T(8,128)(2,1)}, f16[528,2048]{1,0:T(8,128)(2,1)S(1)}, u32[]{:S(2)}, u32[]{:S(2)}) %collective-permute-start.27) | collective-permute-done | bytes 2162720 | tf_op jit(solution)/shard_map/ppermute | solution.py:38
  1049.9 4.1 bitcast_dynamic-update-slice_fusion.10
  (165 shorter events, 99.1 us)
Async XLA Ops:
  7.2 159.6 %all-gather.9.cloned.1.call-start = ((), (), s32[]{:S(2)}) async-start(), calls=%async_computation | async-start | bytes 25165824 | tf_op jit(solution)/shard_map/all_gather | solution.py:41
  102.2 148.0 %all-gather.15.cloned.1.call-start = ((), (), s32[]{:S(2)}) async-start(), calls=%async_computation.3 | async-start | bytes 25165824 | tf_op jit(solution)/shard_map/all_gather | solution.py:41
  109.0 46.9 %collective-permute-start = (f32[3]{0:T(128)S(1)}, f32[3]{0:T(128)S(1)}, u32[]{:S(2)}, u32[]{:S(2)}) collective-permute-start(f32[3]{0:T(128)S(1)} %pad_maximum_fusion), channel_id=1, source_target_pairs={{0,1},{1,0},{2,3},{3,2},{4,5},{5,4},{6,7},{7,6}} | collective-permute-start | bytes 44 | tf_op jit(solution)/shard_map/ppermute | solution.py:38
  156.0 3.8 collective-permute-start.1
  159.9 3.6 collective-permute-start.2
  208.6 93.2 %all-gather.13.cloned.1.call-start = ((), (), s32[]{:S(2)}) async-start(), calls=%async_computation.2 | async-start | bytes 25165824 | tf_op jit(solution)/shard_map/all_gather | solution.py:41
  209.3 200.5 %all-gather.21.cloned.1.call-start = ((), (), s32[]{:S(2)}) async-start(), calls=%async_computation.6 | async-start | bytes 25165824 | tf_op jit(solution)/shard_map/all_gather | solution.py:41
  210.6 91.2 %collective-permute-start.3 = (f16[1024,2048]{1,0:T(8,128)(2,1)}, f16[1024,2048]{1,0:T(8,128)(2,1)}, u32[]{:S(2)}, u32[]{:S(2)}) collective-permute-start(f16[1024,2048]{1,0:T(8,128)(2,1)} %multiply_convert_fusion.1), channel_id=1, source_target_pairs={{0,2},{1,3},{2,0},{3,1},{4,6},{5,7},{6,4},{7,5}} | collective-permute-start | bytes 12582920 | tf_op jit(solution)/shard_map/ppermute | solution.py:38
  363.8 78.9 %all-gather.19.cloned.1.call-start = ((), (), s32[]{:S(2)}) async-start(), calls=%async_computation.5 | async-start | bytes 25165824 | tf_op jit(solution)/shard_map/all_gather | solution.py:41
  385.0 73.1 %all-gather.23.cloned.1.call-start = ((), (), s32[]{:S(2)}) async-start(), calls=%async_computation.7 | async-start | bytes 25165824 | tf_op jit(solution)/shard_map/all_gather | solution.py:41
  385.5 270.5 %all-gather.11.cloned.1.call-start = ((), (), s32[]{:S(2)}) async-start(), calls=%async_computation.1 | async-start | bytes 25165824 | tf_op jit(solution)/shard_map/all_gather | solution.py:41
  386.3 269.8 %all-gather.17.cloned.1.call-start = ((), (), s32[]{:S(2)}) async-start(), calls=%async_computation.4 | async-start | bytes 25165824 | tf_op jit(solution)/shard_map/all_gather | solution.py:41
  394.6 1.2 collective-permute-start.4
  395.9 3.6 collective-permute-start.5
  399.5 3.6 collective-permute-start.6
  427.2 53.2 %collective-permute-start.8 = (f16[1024,1024]{1,0:T(8,128)(2,1)}, f16[1024,1024]{1,0:T(8,128)(2,1)}, u32[]{:S(2)}, u32[]{:S(2)}) collective-permute-start(f16[1024,1024]{1,0:T(8,128)(2,1)} %multiply_convert_fusion.11), channel_id=1, source_target_pairs={{0,2},{1,3},{2,0},{3,1},{4,6},{5,7},{6,4},{7,5}} | collective-permute-start | bytes 6291464 | tf_op jit(solution)/shard_map/ppermute | solution.py:38
  476.8 170.7 %collective-permute-start.10 = (f16[1024,1024]{1,0:T(8,128)(2,1)}, f16[1024,1024]{1,0:T(8,128)(2,1)S(1)}, u32[]{:S(2)}, u32[]{:S(2)}) collective-permute-start(f16[1024,1024]{1,0:T(8,128)(2,1)} %multiply_convert_fusion.8), channel_id=1, source_target_pairs={{0,4},{1,5},{2,6},{3,7},{4,0},{5,1},{6,2},{7,3}} | collective-permute-start | bytes 6291464 | tf_op jit(solution)/shard_map/ppermute | solution.py:38
  478.7 172.8 %collective-permute-start.7 = (f16[1024,1024]{1,0:T(8,128)(2,1)}, f16[1024,1024]{1,0:T(8,128)(2,1)S(1)}, u32[]{:S(2)}, u32[]{:S(2)}) collective-permute-start(f16[1024,1024]{1,0:T(8,128)(2,1)} %multiply_convert_fusion.9), channel_id=1, source_target_pairs={{0,2},{1,3},{2,0},{3,1},{4,6},{5,7},{6,4},{7,5}} | collective-permute-start | bytes 6291464 | tf_op jit(solution)/shard_map/ppermute | solution.py:38
  479.9 90.7 %collective-permute-start.11 = (f16[1024,1024]{1,0:T(8,128)(2,1)}, f16[1024,1024]{1,0:T(8,128)(2,1)}, u32[]{:S(2)}, u32[]{:S(2)}) collective-permute-start(f16[1024,1024]{1,0:T(8,128)(2,1)} %multiply_convert_fusion.10), channel_id=1, source_target_pairs={{0,4},{1,5},{2,6},{3,7},{4,0},{5,1},{6,2},{7,3}} | collective-permute-start | bytes 6291464 | tf_op jit(solution)/shard_map/ppermute | solution.py:38
  493.0 160.1 %collective-permute-start.9 = (f16[1024,1024]{1,0:T(8,128)(2,1)}, f16[1024,1024]{1,0:T(8,128)(2,1)S(1)}, u32[]{:S(2)}, u32[]{:S(2)}) collective-permute-start(f16[1024,1024]{1,0:T(8,128)(2,1)} %add_convert_fusion.4), channel_id=1, source_target_pairs={{0,4},{1,5},{2,6},{3,7},{4,0},{5,1},{6,2},{7,3}} | collective-permute-start | bytes 6291464 | tf_op jit(solution)/shard_map/ppermute | solution.py:38
  584.7 63.7 %collective-permute-start.12 = (f16[1024,1024]{1,0:T(8,128)(2,1)S(1)}, f16[1024,1024]{1,0:T(8,128)(2,1)S(1)}, u32[]{:S(2)}, u32[]{:S(2)}) collective-permute-start(f16[1024,1024]{1,0:T(8,128)(2,1)S(1)} %add_convert_fusion.3), channel_id=1, source_target_pairs={{0,2},{1,3},{2,0},{3,1},{4,6},{5,7},{6,4},{7,5}} | collective-permute-start | bytes 6291464 | tf_op jit(solution)/shard_map/ppermute | solution.py:38
  646.0 171.2 %collective-permute-start.34 = (f16[1024,1024]{1,0:T(8,128)(2,1)}, f16[1024,1024]{1,0:T(8,128)(2,1)}, u32[]{:S(2)}, u32[]{:S(2)}) collective-permute-start(f16[1024,1024]{1,0:T(8,128)(2,1)} %multiply_convert_fusion.4), channel_id=1, source_target_pairs={{0,4},{1,5},{2,6},{3,7},{4,0},{5,1},{6,2},{7,3}} | collective-permute-start | bytes 6291464 | tf_op jit(solution)/shard_map/ppermute | solution.py:38
  647.5 182.3 %collective-permute-start.32 = (f16[1024,1024]{1,0:T(8,128)(2,1)}, f16[1024,1024]{1,0:T(8,128)(2,1)S(1)}, u32[]{:S(2)}, u32[]{:S(2)}) collective-permute-start(f16[1024,1024]{1,0:T(8,128)(2,1)} %multiply_convert_fusion.5), channel_id=1, source_target_pairs={{0,2},{1,3},{2,0},{3,1},{4,6},{5,7},{6,4},{7,5}} | collective-permute-start | bytes 6291464 | tf_op jit(solution)/shard_map/ppermute | solution.py:38
  648.4 112.5 %collective-permute-start.14 = (f16[1024,1024]{1,0:T(8,128)(2,1)}, f16[1024,1024]{1,0:T(8,128)(2,1)}, u32[]{:S(2)}, u32[]{:S(2)}) collective-permute-start(f16[1024,1024]{1,0:T(8,128)(2,1)} %multiply_convert_fusion.6), channel_id=1, source_target_pairs={{0,4},{1,5},{2,6},{3,7},{4,0},{5,1},{6,2},{7,3}} | collective-permute-start | bytes 6291464 | tf_op jit(solution)/shard_map/ppermute | solution.py:38
  651.5 89.8 %collective-permute-start.13 = (f16[1024,1024]{1,0:T(8,128)(2,1)}, f16[1024,1024]{1,0:T(8,128)(2,1)}, u32[]{:S(2)}, u32[]{:S(2)}) collective-permute-start(f16[1024,1024]{1,0:T(8,128)(2,1)} %multiply_convert_fusion.7), channel_id=1, source_target_pairs={{0,2},{1,3},{2,0},{3,1},{4,6},{5,7},{6,4},{7,5}} | collective-permute-start | bytes 6291464 | tf_op jit(solution)/shard_map/ppermute | solution.py:38
  741.2 60.3 %copy-start.1 = (f32[1024,2048]{1,0:T(8,128)}, f32[1024,2048]{1,0:T(8,128)S(1)}, u32[]{:S(2)}) copy-start(f32[1024,2048]{1,0:T(8,128)S(1)} %fusion.48) | copy-start | bytes 25165828
  741.2 93.2 %collective-permute-start.15 = (f32[1024,2048]{1,0:T(8,128)S(1)}, f32[1024,2048]{1,0:T(8,128)S(1)}, u32[]{:S(2)}, u32[]{:S(2)}) collective-permute-start(f32[1024,2048]{1,0:T(8,128)S(1)} %fusion.48), channel_id=1, source_target_pairs={{0,1},{1,0},{2,3},{3,2},{4,5},{5,4},{6,7},{7,6}} | collective-permute-start | bytes 25165832 | tf_op jit(solution)/shard_map/ppermute | solution.py:38
  759.4 70.4 %collective-permute-start.33 = (f16[1024,1024]{1,0:T(8,128)(2,1)}, f16[1024,1024]{1,0:T(8,128)(2,1)}, u32[]{:S(2)}, u32[]{:S(2)}) collective-permute-start(f16[1024,1024]{1,0:T(8,128)(2,1)} %add_convert_fusion.2), channel_id=1, source_target_pairs={{0,4},{1,5},{2,6},{3,7},{4,0},{5,1},{6,2},{7,3}} | collective-permute-start | bytes 6291464 | tf_op jit(solution)/shard_map/ppermute | solution.py:38
  776.0 48.7 %collective-permute-start.35 = (f16[1024,1024]{1,0:T(8,128)(2,1)}, f16[1024,1024]{1,0:T(8,128)(2,1)S(1)}, u32[]{:S(2)}, u32[]{:S(2)}) collective-permute-start(f16[1024,1024]{1,0:T(8,128)(2,1)} %add_convert_fusion.1), channel_id=1, source_target_pairs={{0,2},{1,3},{2,0},{3,1},{4,6},{5,7},{6,4},{7,5}} | collective-permute-start | bytes 6291464 | tf_op jit(solution)/shard_map/ppermute | solution.py:38
  817.2 116.6 %collective-permute-start.30 = (f16[1024,2048]{1,0:T(8,128)(2,1)}, f16[1024,2048]{1,0:T(8,128)(2,1)}, u32[]{:S(2)}, u32[]{:S(2)}) collective-permute-start(f16[1024,2048]{1,0:T(8,128)(2,1)} %multiply_convert_fusion), channel_id=1, source_target_pairs={{0,2},{1,3},{2,0},{3,1},{4,6},{5,7},{6,4},{7,5}} | collective-permute-start | bytes 12582920 | tf_op jit(solution)/shard_map/ppermute | solution.py:38
  824.7 109.6 %collective-permute-start.31 = (f16[1024,2048]{1,0:T(8,128)(2,1)}, f16[1024,2048]{1,0:T(8,128)(2,1)}, u32[]{:S(2)}, u32[]{:S(2)}) collective-permute-start(f16[1024,2048]{1,0:T(8,128)(2,1)} %add_convert_fusion), channel_id=1, source_target_pairs={{0,4},{1,5},{2,6},{3,7},{4,0},{5,1},{6,2},{7,3}} | collective-permute-start | bytes 12582920 | tf_op jit(solution)/shard_map/ppermute | solution.py:38
  897.4 38.1 %slice-start.2 = ((s8[8388608]{0:T(1024)(128)(4,1)}), s8[4194304]{0:T(1024)(128)(4,1)S(1)}, s32[]{:S(2)}) async-start(s8[8388608]{0:T(1024)(128)(4,1)} %bitcast.136), calls=%async_computation.10 | async-start | bytes 8388608
  904.7 57.3 %collective-permute-start.23 = (f16[528,2048]{1,0:T(8,128)(2,1)}, f16[528,2048]{1,0:T(8,128)(2,1)}, u32[]{:S(2)}, u32[]{:S(2)}) collective-permute-start(f16[528,2048]{1,0:T(8,128)(2,1)} %concatenate.23), channel_id=1, source_target_pairs={{0,4},{1,5},{2,6},{3,7},{4,0},{5,1},{6,2},{7,3}} | collective-permute-start | bytes 6488072 | tf_op jit(solution)/shard_map/ppermute | solution.py:38
  906.1 101.2 %collective-permute-start.19 = (f16[528,2048]{1,0:T(8,128)(2,1)}, f16[528,2048]{1,0:T(8,128)(2,1)}, u32[]{:S(2)}, u32[]{:S(2)}) collective-permute-start(f16[528,2048]{1,0:T(8,128)(2,1)} %concatenate.23), channel_id=1, source_target_pairs={{0,2},{1,3},{2,0},{3,1},{4,6},{5,7},{6,4},{7,5}} | collective-permute-start | bytes 6488072 | tf_op jit(solution)/shard_map/ppermute | solution.py:38
  907.0 55.6 %collective-permute-start.16 = (f16[528,2048]{1,0:T(8,128)(2,1)}, f16[528,2048]{1,0:T(8,128)(2,1)}, u32[]{:S(2)}, u32[]{:S(2)}) collective-permute-start(f16[528,2048]{1,0:T(8,128)(2,1)} %concatenate.22), channel_id=1, source_target_pairs={{0,1},{1,0},{2,3},{3,2},{4,5},{5,4},{6,7},{7,6}} | collective-permute-start | bytes 6488072 | tf_op jit(solution)/shard_map/ppermute | solution.py:38
  907.0 28.5 %slice-start.3 = ((s8[8388608]{0:T(1024)(128)(4,1)}), s8[4194304]{0:T(1024)(128)(4,1)S(1)}, s32[]{:S(2)}) async-start(s8[8388608]{0:T(1024)(128)(4,1)} %bitcast.136), calls=%async_computation.11 | async-start | bytes 8388608
  933.8 28.2 %copy-start.3 = (f16[528,2048]{1,0:T(8,128)(2,1)S(1)}, f16[528,2048]{1,0:T(8,128)(2,1)}, u32[]{:S(2)}) copy-start(f16[528,2048]{1,0:T(8,128)(2,1)} %concatenate.22) | copy-start | bytes 6488068
  933.8 74.1 %collective-permute-start.17 = (f16[528,2048]{1,0:T(8,128)(2,1)}, f16[528,2048]{1,0:T(8,128)(2,1)S(1)}, u32[]{:S(2)}, u32[]{:S(2)}) collective-permute-start(f16[528,2048]{1,0:T(8,128)(2,1)} %concatenate.23), channel_id=1, source_target_pairs={{0,1},{1,0},{2,3},{3,2},{4,5},{5,4},{6,7},{7,6}} | collective-permute-start | bytes 6488072 | tf_op jit(solution)/shard_map/ppermute | solution.py:38
  934.4 72.9 %collective-permute-start.18 = (f16[528,2048]{1,0:T(8,128)(2,1)}, f16[528,2048]{1,0:T(8,128)(2,1)S(1)}, u32[]{:S(2)}, u32[]{:S(2)}) collective-permute-start(f16[528,2048]{1,0:T(8,128)(2,1)} %concatenate.22), channel_id=1, source_target_pairs={{0,2},{1,3},{2,0},{3,1},{4,6},{5,7},{6,4},{7,5}} | collective-permute-start | bytes 6488072 | tf_op jit(solution)/shard_map/ppermute | solution.py:38
  962.0 52.0 %collective-permute-start.22 = (f16[528,2048]{1,0:T(8,128)(2,1)S(1)}, f16[528,2048]{1,0:T(8,128)(2,1)S(1)}, u32[]{:S(2)}, u32[]{:S(2)}) collective-permute-start(f16[528,2048]{1,0:T(8,128)(2,1)S(1)} %copy-done.3), channel_id=1, source_target_pairs={{0,4},{1,5},{2,6},{3,7},{4,0},{5,1},{6,2},{7,3}} | collective-permute-start | bytes 6488072 | tf_op jit(solution)/shard_map/ppermute | solution.py:38
  962.6 87.3 %collective-permute-start.27 = (f16[528,2048]{1,0:T(8,128)(2,1)}, f16[528,2048]{1,0:T(8,128)(2,1)S(1)}, u32[]{:S(2)}, u32[]{:S(2)}) collective-permute-start(f16[528,2048]{1,0:T(8,128)(2,1)} %collective-permute-done.23), channel_id=1, source_target_pairs={{0,2},{1,3},{2,0},{3,1},{4,6},{5,7},{6,4},{7,5}} | collective-permute-start | bytes 6488072 | tf_op jit(solution)/shard_map/ppermute | solution.py:38
  1007.3 46.7 %collective-permute-start.25 = (f16[528,2048]{1,0:T(8,128)(2,1)}, f16[528,2048]{1,0:T(8,128)(2,1)S(1)}, u32[]{:S(2)}, u32[]{:S(2)}) collective-permute-start(f16[528,2048]{1,0:T(8,128)(2,1)} %collective-permute-done.23), channel_id=1, source_target_pairs={{0,1},{1,0},{2,3},{3,2},{4,5},{5,4},{6,7},{7,6}} | collective-permute-start | bytes 6488072 | tf_op jit(solution)/shard_map/ppermute | solution.py:38
  1007.4 49.5 %collective-permute-start.26 = (f16[528,2048]{1,0:T(8,128)(2,1)S(1)}, f16[528,2048]{1,0:T(8,128)(2,1)S(1)}, u32[]{:S(2)}, u32[]{:S(2)}) collective-permute-start(f16[528,2048]{1,0:T(8,128)(2,1)S(1)} %collective-permute-done.18), channel_id=1, source_target_pairs={{0,4},{1,5},{2,6},{3,7},{4,0},{5,1},{6,2},{7,3}} | collective-permute-start | bytes 6488072 | tf_op jit(solution)/shard_map/ppermute | solution.py:38
  1007.9 48.9 %collective-permute-start.21 = (f16[528,2048]{1,0:T(8,128)(2,1)}, f16[528,2048]{1,0:T(8,128)(2,1)S(1)}, u32[]{:S(2)}, u32[]{:S(2)}) collective-permute-start(f16[528,2048]{1,0:T(8,128)(2,1)} %collective-permute-done.19), channel_id=1, source_target_pairs={{0,1},{1,0},{2,3},{3,2},{4,5},{5,4},{6,7},{7,6}} | collective-permute-start | bytes 6488072 | tf_op jit(solution)/shard_map/ppermute | solution.py:38
  1014.0 42.9 %collective-permute-start.24 = (f16[528,2048]{1,0:T(8,128)(2,1)S(1)}, f16[528,2048]{1,0:T(8,128)(2,1)S(1)}, u32[]{:S(2)}, u32[]{:S(2)}) collective-permute-start(f16[528,2048]{1,0:T(8,128)(2,1)S(1)} %collective-permute-done.22), channel_id=1, source_target_pairs={{0,1},{1,0},{2,3},{3,2},{4,5},{5,4},{6,7},{7,6}} | collective-permute-start | bytes 6488072 | tf_op jit(solution)/shard_map/ppermute | solution.py:38
  1049.9 7.0 collective-permute-start.20
  1054.1 24.7 %collective-permute-start.29 = (f16[528,2048]{1,0:T(8,128)(2,1)S(1)}, f16[528,2048]{1,0:T(8,128)(2,1)S(1)}, u32[]{:S(2)}, u32[]{:S(2)}) collective-permute-start(f16[528,2048]{1,0:T(8,128)(2,1)S(1)} %collective-permute-done.27), channel_id=1, source_target_pairs={{0,1},{1,0},{2,3},{3,2},{4,5},{5,4},{6,7},{7,6}} | collective-permute-start | bytes 6488072 | tf_op jit(solution)/shard_map/ppermute | solution.py:38
  1056.8 21.9 %collective-permute-start.28 = (f16[528,2048]{1,0:T(8,128)(2,1)S(1)}, f16[528,2048]{1,0:T(8,128)(2,1)S(1)}, u32[]{:S(2)}, u32[]{:S(2)}) collective-permute-start(f16[528,2048]{1,0:T(8,128)(2,1)S(1)} %collective-permute-done.26), channel_id=1, source_target_pairs={{0,1},{1,0},{2,3},{3,2},{4,5},{5,4},{6,7},{7,6}} | collective-permute-start | bytes 6488072 | tf_op jit(solution)/shard_map/ppermute | solution.py:38
  (9 other events, 156.6 us)
Sparse Core Ops, SparseCore 0:
  102.3 30.0 all-gather.8
  208.7 28.7 all-gather.14
  239.1 28.4 all-gather.12
  363.9 28.4 all-gather.20
  393.8 28.4 all-gather.18
  423.7 28.4 all-gather.22
  453.7 28.4 all-gather.10
  483.7 28.4 all-gather.16
